TPU v7x, 512 devices: a whole 4x4x16 slice. The times are simulated.
512 devices in a mesh: rows: 128 (over x, z_lo, y), cols: 4 (over z_hi, core).
Axes of the slice: x: 4, y: 4, z: 16 (z_hi: 2, z_lo: 8; z = z_hi * 8 + z_lo), core: 2. Of those that a mesh axis runs over, the one named last changes fastest.
Arguments:
- coords: int32 [8, 262144], P(None, ('rows', 'cols')), may hold values from 0 to 4095
- probes: float32 [64, 262144], P(None, ('rows', 'cols')), may hold values from -6 to 6
- lengthscales: float32 [8], replicated, may hold values from 0.15 to 0.25
- amplitude: float32 [1], replicated, may hold values from 0.1 to 0.3
- landmarks: float32 [254, 8, 128], replicated, may hold values from 0 to 1
- coupling: float32 [128, 128], replicated, may hold values from -0.5 to 0.5
Outputs:
- products: float32 [2, 64, 262144], P(None, None, ('rows', 'cols'))
All inputs are finite; a program needn't handle non-finite values.
Results may differ from a plain program's by a relative error of at most 0.0025.
Values may be sent and summed in bfloat16 or wider, within the bound.
No kernel may reach another device: no remote copies, remote signals or barrier semaphores. Data moves between devices by JAX's collectives and lax.ppermute only.
A program may use at most 64 MiB of HBM per device.

v0:
```python
import math

import jax
import jax.numpy as jnp
from jax import lax
from jax.experimental import pallas as pl
from jax.experimental.pallas import tpu as pltpu
from jax.sharding import Mesh, PartitionSpec as P


LEVELS = 7
PROBES = 64
RANK = 128
HALF = RANK // 2
QUARTER = PROBES // 4
SPAN = 128
WIDTH = 512
TRANSFER = 80
LANES = 1024
BLOCK = 256
KEPT = WIDTH + RANK
ALL_SPANS = ((0, 256), (256, 512), (512, 768), (768, 1024))
LATE_SPANS = ((0, 256), (256, 512), (512, 640))
ROOT = math.sqrt(math.log2(math.e))
TWO_LN2 = 2.0 * math.log(2.0)
F32 = jnp.float32
BF16 = jnp.bfloat16
I16 = jnp.int16
FINE = 2.0**26
OCTAVES = 44.0
VMEM = pl.BlockSpec(memory_space=pltpu.VMEM)
ROOM = pltpu.CompilerParams(vmem_limit_bytes=16 * 2**20)
SMEM = pl.BlockSpec(memory_space=pltpu.SMEM)


def cost(flops, moved):
    return pl.CostEstimate(flops=flops, bytes_accessed=moved, transcendentals=0)


def row_index():
    z = lax.axis_index("zh") * 2 + lax.axis_index("zl")
    return lax.axis_index("x") * 32 + z * 4 + lax.axis_index("y")


def split3(value):
    first = value.astype(BF16).astype(F32)
    rest = value - first
    second = rest.astype(BF16).astype(F32)
    third = (rest - second).astype(BF16).astype(F32)
    return first, second, third


def norms(value):
    return -0.5 * jnp.sum(value * value, axis=0, keepdims=True)


def stacked(parts, rows):
    width = parts[0].shape[1]
    index = lax.broadcasted_iota(jnp.int32, (8, width), 0)
    held = jnp.zeros((8, width), F32)
    for k, row in enumerate(rows):
        held = jnp.where(index == k, row, held)
    zeros = jnp.zeros((SPAN - 56, width), F32)
    return jnp.concatenate(list(parts) + [held, zeros], axis=0)


def left_form(value, extra):
    one, two, three = split3(value)
    n1, n2, n3 = split3(norms(value) + extra)
    return stacked((one, one, two, one, three, two), (1.0, 1.0, 1.0, n1, n2, n3))


def right_form(value, extra):
    one, two, three = split3(value)
    n1, n2, n3 = split3(norms(value) + extra)
    return stacked((one, two, one, three, one, two), (n1, n2, n3, 1.0, 1.0, 1.0))


def points_of(message, inverse):
    high = message[PROBES : PROBES + 8, :].astype(F32)
    low = message[PROBES + 8 : PROBES + 16, :].astype(F32)
    return ((high * 64.0 + low) * (1.0 / 4096.0) - 0.5) * inverse


def kernel_pair(exponent, log_strength):
    kern = jnp.exp2(exponent)
    return kern, kern * (TWO_LN2 * log_strength - TWO_LN2 * exponent)


def halved(value):
    top = value.astype(BF16)
    return top, (value - top.astype(F32)).astype(BF16)


def encode(value):
    grade = jnp.log(1.0 + jnp.abs(value) * FINE) * (32767.0 / (OCTAVES * math.log(2.0))) + 0.5
    return jnp.where(value < 0.0, -grade, grade).astype(jnp.int32).astype(jnp.int16)


def decode(code):
    grade = code.astype(jnp.int32).astype(F32)
    size = (jnp.exp2(jnp.abs(grade) * (OCTAVES / 32767.0)) - 1.0) * (1.0 / FINE)
    return jnp.where(grade < 0.0, -size, size)


def prepare_kernel(
    coords_ref, probes_ref, marks_ref, scales_ref, strength_ref,
    out_ref, picked_ref, facts_ref, coords_buf, probes_buf, scales_buf, sem,
):
    row = row_index()
    copies = [
        pltpu.make_async_copy(probes_ref, probes_buf, sem.at[0]),
        pltpu.make_async_copy(coords_ref, coords_buf, sem.at[1]),
        pltpu.make_async_copy(scales_ref, scales_buf, sem.at[2 + LEVELS]),
    ]
    for level in range(LEVELS):
        node = 2 ** (LEVELS - level) - 2 + jnp.right_shift(row, level)
        copies.append(pltpu.make_async_copy(marks_ref.at[node], picked_ref.at[level], sem.at[2 + level]))
    for copy in copies:
        copy.start()
    for copy in copies:
        copy.wait()
    coords = coords_buf[...]
    high = jnp.right_shift(coords, 6)
    low = coords - high * 64
    out_ref[0:PROBES, :] = probes_buf[...].astype(BF16)
    both = jnp.concatenate([high.astype(F32), low.astype(F32)], axis=0)
    out_ref[PROBES:TRANSFER, :] = both.astype(BF16)
    place = lax.broadcasted_iota(jnp.int32, (8, 128), 0)
    held = jnp.full((8, 128), scales_buf[0], F32)
    for k in range(1, 8):
        held = jnp.where(place == k, scales_buf[k], held)
    facts_ref[0:8, :] = ROOT / held
    facts_ref[8:16, :] = jnp.log(jnp.full((8, 128), strength_ref[0], F32)) * math.log2(math.e)


def accumulate(message_ref, facts_ref, right_ref, sums, spans, fresh):
    message = message_ref[...]
    left = left_form(points_of(message, facts_ref[0:8, 0:1]), 0.0).T.astype(BF16)
    for block in range(WIDTH // BLOCK):
        rows = left[block * BLOCK : (block + 1) * BLOCK, :]
        signs = message[0:PROBES, block * BLOCK : (block + 1) * BLOCK]
        for start, stop in spans:
            exponent = jnp.dot(rows, right_ref[:, start:stop], preferred_element_type=F32)
            for which, value in enumerate(kernel_pair(exponent, facts_ref[8:9, 0:1])):
                top, rest = halved(value)
                total = jnp.dot(signs, top, preferred_element_type=F32)
                if start >= WIDTH:
                    total = total + jnp.dot(signs, rest, preferred_element_type=F32)
                if fresh and block == 0:
                    sums[which, :, start:stop] = total
                else:
                    sums[which, :, start:stop] += total


def unit_of(sums, level):
    at = WIDTH + level * HALF
    return encode(jnp.concatenate([sums[0, :, at : at + HALF], sums[1, :, at : at + HALF]], axis=1))


def own_kernel(own_ref, facts_ref, marks_ref, held_ref, right_ref):
    core = lax.axis_index("c")
    inverse = facts_ref[0:8, 0:1]
    own = points_of(own_ref[...], inverse)
    halves = []
    for level in range(LEVELS):
        mark = (marks_ref[level] - 0.5) * inverse
        halves.append(jnp.where(core == 0, mark[:, :HALF], mark[:, HALF:]))
    halves.append(jnp.zeros((8, HALF), F32))
    columns = jnp.concatenate([own] + halves, axis=1)
    right_ref[...] = right_form(columns, facts_ref[8:9, 0:1]).astype(BF16)
    accumulate(own_ref, facts_ref, right_ref, held_ref, ALL_SPANS, True)


def factor_kernel(facts_ref, marks_ref, right_ref, factor_ref):
    inverse = facts_ref[0:8, 0:1]
    right = right_ref[:, :WIDTH]
    for level in range(LEVELS):
        turned = left_form((marks_ref[level] - 0.5) * inverse, 0.0).T.astype(BF16)
        exponent = jnp.dot(turned, right, preferred_element_type=F32)
        for which, value in enumerate(kernel_pair(exponent, facts_ref[8:9, 0:1])):
            factor_ref[which, level * RANK : (level + 1) * RANK, :] = value.astype(BF16)


def near_kernel(other_ref, facts_ref, held_ref, right_ref, kept_ref, line_ref, sums):
    zl = lax.axis_index("zl")
    sums[...] = held_ref[...]
    accumulate(other_ref, facts_ref, right_ref, sums, ALL_SPANS, False)
    kept_ref[...] = sums[:, :, :KEPT]
    units = [unit_of(sums, level) for level in range(2, LEVELS)]
    blank = jnp.zeros((QUARTER, 128), I16)
    for at in range(4):
        part = slice(at * QUARTER, (at + 1) * QUARTER)
        higher = [unit[part] for unit in units[1:]]
        line_ref[zl * 4 + at] = jnp.concatenate([blank] + higher, axis=0)
        line_ref[(1 - zl) * 4 + at] = jnp.concatenate([units[0][part]] + higher, axis=0)


def added(parts):
    while len(parts) > 1:
        parts = [a + b for a, b in zip(parts[::2], parts[1::2])]
    return parts[0]


def line_kernel(got_ref, out_ref):
    x = lax.axis_index("x")
    zh = lax.axis_index("zh")
    zl = lax.axis_index("zl")
    two = encode(added([decode(got_ref[(1 - zl) * 4 + at, 0:QUARTER]) for at in range(4)]))
    packed = encode(added([decode(got_ref[at, QUARTER:]) for at in range(8)]))
    parts = [packed[at * QUARTER : (at + 1) * QUARTER] for at in range(4)]
    for aside in range(4):
        for apart in range(4):
            place = jnp.bitwise_xor(x, aside) * 8 + jnp.bitwise_xor(zh, apart) * 2
            if aside > 0:
                piece = parts[1 + aside.bit_length()]
            elif apart > 0:
                piece = parts[apart.bit_length() - 1]
            else:
                piece = two
            for half in range(2):
                out_ref[place + half] = piece


def far_kernel(far_ref, facts_ref, kept_ref, right_ref, out_ref):
    out_ref[...] = kept_ref[...]
    accumulate(far_ref, facts_ref, right_ref, out_ref, LATE_SPANS, False)


def cross_kernel(cross_ref, facts_ref, kept_ref, right_ref, diagonal_ref, low_ref, sums):
    y = lax.axis_index("y")
    sums[...] = kept_ref[...]
    accumulate(cross_ref, facts_ref, right_ref, sums, LATE_SPANS, False)
    diagonal_ref[...] = sums[:, :, :WIDTH]
    units = [unit_of(sums, level) for level in range(2)]
    low_ref[y] = jnp.zeros((PROBES, 128), I16)
    for apart, level in ((1, 0), (2, 1), (3, 1)):
        low_ref[jnp.bitwise_xor(y, apart)] = units[level]


def depth_kernel(got_ref, low_ref, out_ref):
    x = lax.axis_index("x")
    zh = lax.axis_index("zh")

    def total(asides, aparts):
        return added([
            decode(got_ref[jnp.bitwise_xor(x, aside) * 8 + jnp.bitwise_xor(zh, apart) * 2 + half])
            for aside in asides for apart in aparts for half in range(2)
        ])

    found = [
        total((0,), (0,)),
        total((0,), (1,)),
        total((0,), (2, 3)),
        total((1,), range(4)),
        total((2, 3), range(4)),
    ]
    packed = encode(jnp.concatenate(found, axis=0))
    for at in range(4):
        for core in range(2):
            out_ref[2 * at + core, 0:PROBES] = low_ref[at]
            out_ref[2 * at + core, PROBES:] = packed


def final_kernel(got_ref, factor_ref, coupling_ref, diagonal_ref, out_ref, sibling):
    y = lax.axis_index("y")
    row = row_index()
    for core in range(2):
        lanes = slice(core * 128, core * 128 + 128)
        sibling[0:PROBES, lanes] = decode(got_ref[jnp.bitwise_xor(y, 1) * 2 + core, 0:PROBES])
        pair = decode(got_ref[jnp.bitwise_xor(y, 2) * 2 + core, 0:PROBES])
        pair = pair + decode(got_ref[jnp.bitwise_xor(y, 3) * 2 + core, 0:PROBES])
        sibling[PROBES : 2 * PROBES, lanes] = pair
        for level in range(2, LEVELS):
            for at in range(4):
                start = level * PROBES + at * QUARTER
                source = PROBES + (level - 2) * QUARTER
                sibling[start : start + QUARTER, lanes] = decode(got_ref[2 * at + core, source : source + QUARTER])
    coupling = coupling_ref[...]
    blank = jnp.zeros((HALF, RANK), F32)

    def spread(core_matrix):
        rows = []
        for core in range(2):
            part = core_matrix[core * HALF : (core + 1) * HALF, :]
            rows.append(jnp.concatenate([part, blank], axis=1))
            rows.append(jnp.concatenate([blank, part], axis=1))
        whole = jnp.concatenate(rows, axis=0)
        return halved(whole)

    values, remainders = halved(sibling[...])
    results = []
    for matrix in (coupling.T, coupling):
        top, rest = spread(matrix)
        results.append(
            jnp.dot(values, top, preferred_element_type=F32)
            + jnp.dot(values, rest, preferred_element_type=F32)
            + jnp.dot(remainders, top, preferred_element_type=F32)
        )
    heads = []
    for level in range(LEVELS):
        rows = slice(level * PROBES, (level + 1) * PROBES)
        left = jnp.bitwise_and(jnp.right_shift(row, level), 1) == 0
        heads.append(jnp.where(left, results[0][rows], results[1][rows]))
    firsts = jnp.concatenate([head[:, :RANK] for head in heads], axis=1)
    seconds = jnp.concatenate([head[:, RANK:] for head in heads], axis=1)
    top, rest = halved(jnp.concatenate([firsts, seconds], axis=0))
    stack = jnp.concatenate([top, rest], axis=0)
    on_kern = jnp.dot(stack, factor_ref[0], preferred_element_type=F32)
    pair = jnp.concatenate([top[:PROBES], rest[:PROBES]], axis=0)
    on_slope = jnp.dot(pair, factor_ref[1], preferred_element_type=F32)
    on_kern = on_kern[: 2 * PROBES] + on_kern[2 * PROBES :]
    on_slope = on_slope[:PROBES] + on_slope[PROBES:]
    out_ref[0] = diagonal_ref[0] + on_kern[:PROBES]
    out_ref[1] = diagonal_ref[1] + (on_kern[PROBES:] + on_slope)


def stay(array):
    return pltpu.with_memory_space_constraint(array, pltpu.HBM)


def swap(value, axis):
    return lax.ppermute(value, axis, [(0, 1), (1, 0)])


def exchange(value, axes):
    return lax.all_to_all(value, axes, 0, 0, tiled=True)


def on_device(coords, probes, lengthscales, amplitude, landmarks, coupling):
    message, marks, facts = pl.pallas_call(
        prepare_kernel,
        out_shape=(
            jax.ShapeDtypeStruct((TRANSFER, WIDTH), BF16),
            jax.ShapeDtypeStruct((LEVELS, 8, RANK), F32),
            jax.ShapeDtypeStruct((16, 128), F32),
        ),
        in_specs=[pl.BlockSpec(memory_space=pltpu.HBM)] * 4 + [SMEM],
        out_specs=(VMEM, VMEM, VMEM),
        scratch_shapes=[
            pltpu.VMEM((8, WIDTH), jnp.int32),
            pltpu.VMEM((PROBES, WIDTH), F32),
            pltpu.SMEM((8,), F32),
            pltpu.SemaphoreType.DMA((3 + LEVELS,)),
        ],
        compiler_params=ROOM,
        cost_estimate=cost(10**5, 2 * 10**5),
        name="prepare",
    )(*[stay(array) for array in (coords, probes, landmarks, lengthscales)], amplitude)
    far = swap(message, "h")
    other = swap(message, "c")
    held, right = pl.pallas_call(
        own_kernel,
        out_shape=(
            jax.ShapeDtypeStruct((2, PROBES, LANES), F32),
            jax.ShapeDtypeStruct((SPAN, LANES), BF16),
        ),
        in_specs=[VMEM] * 3,
        out_specs=(VMEM, VMEM),
        compiler_params=ROOM,
        cost_estimate=cost(10**9, 2 * 10**6),
        name="own",
    )(message, facts, marks)
    kept, line = pl.pallas_call(
        near_kernel,
        out_shape=(
            jax.ShapeDtypeStruct((2, PROBES, KEPT), F32),
            jax.ShapeDtypeStruct((8, 5 * QUARTER, 128), I16),
        ),
        in_specs=[VMEM] * 4,
        out_specs=(VMEM, VMEM),
        scratch_shapes=[pltpu.VMEM((2, PROBES, LANES), F32)],
        compiler_params=ROOM,
        cost_estimate=cost(10**9, 2 * 10**6),
        name="near",
    )(other, facts, held, right)
    line = exchange(line, ("zl", "y"))
    deep = pl.pallas_call(
        line_kernel,
        out_shape=jax.ShapeDtypeStruct((32, QUARTER, 128), I16),
        in_specs=[VMEM],
        out_specs=VMEM,
        compiler_params=ROOM,
        cost_estimate=cost(10**5, 3 * 10**5),
        name="line",
    )(line)
    deep = exchange(deep, ("x", "zh", "h"))
    cross = swap(far, "c")
    kept = pl.pallas_call(
        far_kernel,
        out_shape=jax.ShapeDtypeStruct((2, PROBES, KEPT), F32),
        in_specs=[VMEM] * 4,
        out_specs=VMEM,
        compiler_params=ROOM,
        cost_estimate=cost(10**9, 2 * 10**6),
        name="far",
    )(far, facts, kept, right)
    diagonal, low = pl.pallas_call(
        cross_kernel,
        out_shape=(
            jax.ShapeDtypeStruct((2, PROBES, WIDTH), F32),
            jax.ShapeDtypeStruct((4, PROBES, 128), I16),
        ),
        in_specs=[VMEM] * 4,
        out_specs=(VMEM, VMEM),
        scratch_shapes=[pltpu.VMEM((2, PROBES, KEPT), F32)],
        compiler_params=ROOM,
        cost_estimate=cost(10**9, 2 * 10**6),
        name="cross",
    )(cross, facts, kept, right)
    factor = pl.pallas_call(
        factor_kernel,
        out_shape=jax.ShapeDtypeStruct((2, LEVELS * RANK, WIDTH), BF16),
        in_specs=[VMEM] * 3,
        out_specs=VMEM,
        compiler_params=ROOM,
        cost_estimate=cost(10**9, 3 * 10**6),
        name="factor",
    )(facts, marks, right)
    wide = pl.pallas_call(
        depth_kernel,
        out_shape=jax.ShapeDtypeStruct((8, PROBES + 5 * QUARTER, 128), I16),
        in_specs=[VMEM] * 2,
        out_specs=VMEM,
        compiler_params=ROOM,
        cost_estimate=cost(10**5, 5 * 10**5),
        name="depth",
    )(deep, low)
    wide = exchange(wide, ("y", "c"))
    return pl.pallas_call(
        final_kernel,
        out_shape=jax.ShapeDtypeStruct((2, PROBES, WIDTH), F32),
        in_specs=[VMEM] * 4,
        out_specs=VMEM,
        scratch_shapes=[pltpu.VMEM((LEVELS * PROBES, 2 * RANK), F32)],
        compiler_params=ROOM,
        cost_estimate=cost(10**9, 3 * 10**6),
        name="final",
    )(wide, factor, coupling, diagonal)


def solution(mesh):
    fine = Mesh(mesh.devices.reshape(4, 4, 2, 4, 2, 2), ("x", "zh", "zl", "y", "h", "c"))
    every = ("x", "zh", "zl", "y", "h", "c")
    in_specs = (P(None, every), P(None, every), P(), P(), P(), P())
    return jax.shard_map(
        on_device, mesh=fine, in_specs=in_specs, out_specs=P(None, None, every), check_vma=False
    )
```

profile of v0, /device:TPU:1, one launch (start us, length us, event | category | flops | bytes accessed | tf_op | source)
XLA Modules:
  0.0 76.8 jit_solution(13293288598377939783)
XLA Ops:
  0.7 1.0 %prepare.1 = (bf16[80,512]{1,0:T(8,128)(2,1)S(1)}, f32[7,8,128]{2,1,0:T(8,128)S(1)}, f32[16,128]{1,0:T(8,128)S(1)}) custom-call(s32[8,512]{1,0:T(8,128)} %coords_ref.1, f32[64,512]{1,0:T(8,128)} %probes_ref.1, f32[254,8,128]{2,1,0:T(8,128)} %marks_ref.1, f32[8]{0:T(128)} %scales_ref.1, f32[1]{0:T(128)S(6)} %copy.7.strength_ref), custom_call_target="tpu_custom_call" | custom-call | flops 100000 | bytes 200000 | tf_op jit(solution)/shard_map/prepare/pallas_call | solution.py:331
  1.7 8.7 %collective-permute-start = (bf16[80,512]{1,0:T(8,128)(2,1)S(1)}, bf16[80,512]{1,0:T(8,128)(2,1)S(1)}, u32[]{:S(2)}, u32[]{:S(2)}) collective-permute-start(bf16[80,512]{1,0:T(8,128)(2,1)S(1)} %get-tuple-element.14.own_ref), channel_id=1, source_target_pairs={{0,1},{1,0},{2,3},{3,2},{4,5},{5,4},{6,7},{7,6},{8,9},{9,8},{10,11... | collective-permute-start | bytes 245768 | tf_op jit(solution)/shard_map/ppermute | solution.py:323
  10.4 1.7 %own.1 = (f32[2,64,1024]{2,1,0:T(8,128)S(1)}, bf16[128,1024]{1,0:T(8,128)(2,1)S(1)}) custom-call(bf16[80,512]{1,0:T(8,128)(2,1)S(1)} %get-tuple-element.14.own_ref, f32[16,128]{1,0:T(8,128)S(1)} %get-tuple-element.15.facts_ref, f32[7,8,128]{2,1,0:T(8,128)S(1)} %get-tuple-element.16.marks_ref), custom_call_target="tpu_custom_call" | custom-call | flops 1000000000 | bytes 2000000 | tf_op jit(solution)/shard_map/own/pallas_call | solution.py:352
  12.2 0.0 collective-permute-done.other_ref
  12.2 1.8 %near.1 = (f32[2,64,640]{2,1,0:T(8,128)S(1)}, s16[8,80,128]{2,1,0:T(8,128)(2,1)S(1)}) custom-call(bf16[80,512]{1,0:T(8,128)(2,1)S(1)} %collective-permute-done.other_ref, f32[16,128]{1,0:T(8,128)S(1)} %get-tuple-element.15.facts_ref, f32[2,64,1024]{2,1,0:T(8,128)S(1)} %get-tuple-element.17.held_ref, bf16[128,1024]{1,0:T(8,128)(2,1)S(1)} %get-tuple-element.18.right_ref), custom_call_target="tpu_custom_call" | custom-call | flops 1000000000 | bytes 2000000 | tf_op jit(solution)/shard_map/near/pallas_call | solution.py:364
  14.0 8.0 %all_to_all.15.got_ref = s16[8,80,128]{2,1,0:T(8,128)(2,1)S(1)} all-to-all(s16[8,80,128]{2,1,0:T(8,128)(2,1)S(1)} %get-tuple-element.19), channel_id=1, replica_groups=mesh['x'=4,'zh'=4,'zl'=2,'y'=4,'h'=2,'c'=2] {'zl','y'}, dimensions={0} | all-to-all | bytes 327680 | tf_op jit(solution)/shard_map/all_to_all | solution.py:327
  22.0 0.8 %line.1 = s16[32,16,128]{2,1,0:T(8,128)(2,1)} custom-call(s16[8,80,128]{2,1,0:T(8,128)(2,1)S(1)} %all_to_all.15.got_ref), custom_call_target="tpu_custom_call" | custom-call | flops 100000 | bytes 300000 | tf_op jit(solution)/shard_map/line/pallas_call | solution.py:378
  22.8 14.3 %all-to-all-start.1 = ((s16[32,16,128]{2,1,0:T(8,128)(2,1)}), s16[32,16,128]{2,1,0:T(8,128)(2,1)S(1)}, u32[]{:S(2)}, u32[]{:S(2)}) async-start(s16[32,16,128]{2,1,0:T(8,128)(2,1)} %line.1), calls=%async_computation.1 | async-start | bytes 262144 | tf_op jit(solution)/shard_map/all_to_all | solution.py:327
  37.2 11.9 %collective-permute-start.1 = (bf16[80,512]{1,0:T(8,128)(2,1)S(1)}, bf16[80,512]{1,0:T(8,128)(2,1)S(1)}, u32[]{:S(2)}, u32[]{:S(2)}) collective-permute-start(bf16[80,512]{1,0:T(8,128)(2,1)S(1)} %get-tuple-element.14.own_ref), channel_id=1, source_target_pairs={{0,2},{2,0},{1,3},{3,1},{4,6},{6,4},{5,7},{7,5},{8,10},{10,8},{9,1... | collective-permute-start | bytes 245768 | tf_op jit(solution)/shard_map/ppermute | solution.py:323
  49.0 6.2 %collective-permute-done.1.far_ref = bf16[80,512]{1,0:T(8,128)(2,1)S(1)} collective-permute-done((bf16[80,512]{1,0:T(8,128)(2,1)S(1)}, bf16[80,512]{1,0:T(8,128)(2,1)S(1)}, u32[]{:S(2)}, u32[]{:S(2)}) %collective-permute-start.1) | collective-permute-done | bytes 81952 | tf_op jit(solution)/shard_map/ppermute | solution.py:323
  55.2 4.8 %collective-permute-start.2 = (bf16[80,512]{1,0:T(8,128)(2,1)S(1)}, bf16[80,512]{1,0:T(8,128)(2,1)S(1)}, u32[]{:S(2)}, u32[]{:S(2)}) collective-permute-start(bf16[80,512]{1,0:T(8,128)(2,1)S(1)} %collective-permute-done.1.far_ref), channel_id=1, source_target_pairs={{0,1},{1,0},{2,3},{3,2},{4,5},{5,4},{6,7},{7,6},{8,9},{9,8},{10,11... | collective-permute-start | bytes 245768 | tf_op jit(solution)/shard_map/ppermute | solution.py:323
  60.0 1.0 %far.1.kept_ref = f32[2,64,640]{2,1,0:T(8,128)S(1)} custom-call(bf16[80,512]{1,0:T(8,128)(2,1)S(1)} %collective-permute-done.1.far_ref, f32[16,128]{1,0:T(8,128)S(1)} %get-tuple-element.15.facts_ref, f32[2,64,640]{2,1,0:T(8,128)S(1)} %get-tuple-element.20.kept_ref, bf16[128,1024]{1,0:T(8,128)(2,1)S(1)} %get-tuple-element.18.right_ref), custom_call_target="tpu_custom_call" | custom-call | flops 1000000000 | bytes 2000000 | tf_op jit(solution)/shard_map/far/pallas_call | solution.py:389
  61.0 0.0 collective-permute-done.2.cross_ref
  61.1 1.1 %cross.1 = (f32[2,64,512]{2,1,0:T(8,128)S(1)}, s16[4,64,128]{2,1,0:T(8,128)(2,1)S(1)}) custom-call(bf16[80,512]{1,0:T(8,128)(2,1)S(1)} %collective-permute-done.2.cross_ref, f32[16,128]{1,0:T(8,128)S(1)} %get-tuple-element.15.facts_ref, f32[2,64,640]{2,1,0:T(8,128)S(1)} %far.1.kept_ref, bf16[128,1024]{1,0:T(8,128)(2,1)S(1)} %get-tuple-element.18.right_ref), custom_call_target="tpu_custom_call" | custom-call | flops 1000000000 | bytes 2000000 | tf_op jit(solution)/shard_map/cross/pallas_call | solution.py:398
  62.2 0.0 all-to-all-done.1.got_ref
  62.2 0.9 %depth.1 = s16[8,144,128]{2,1,0:T(8,128)(2,1)} custom-call(s16[32,16,128]{2,1,0:T(8,128)(2,1)S(1)} %all-to-all-done.1.got_ref, s16[4,64,128]{2,1,0:T(8,128)(2,1)S(1)} %get-tuple-element.21.low_ref), custom_call_target="tpu_custom_call" | custom-call | flops 100000 | bytes 500000 | tf_op jit(solution)/shard_map/depth/pallas_call | solution.py:420
  63.0 5.2 %all-to-all-start.2 = ((s16[8,144,128]{2,1,0:T(8,128)(2,1)}), s16[8,144,128]{2,1,0:T(8,128)(2,1)S(1)}, u32[]{:S(2)}, u32[]{:S(2)}) async-start(s16[8,144,128]{2,1,0:T(8,128)(2,1)} %depth.1), calls=%async_computation.2 | async-start | bytes 589824 | tf_op jit(solution)/shard_map/all_to_all | solution.py:327
  68.2 0.0 copy-start
  68.2 0.6 factor.1.factor_ref
  68.9 6.1 %all-to-all-done.2.got_ref = s16[8,144,128]{2,1,0:T(8,128)(2,1)S(1)} async-done(((s16[8,144,128]{2,1,0:T(8,128)(2,1)}), s16[8,144,128]{2,1,0:T(8,128)(2,1)S(1)}, u32[]{:S(2)}, u32[]{:S(2)}) %all-to-all-start.2) | async-done | bytes 294944 | tf_op jit(solution)/shard_map/all_to_all | solution.py:327
  75.0 0.0 copy-done
  75.0 1.8 %final.1 = f32[2,64,512]{2,1,0:T(8,128)} custom-call(s16[8,144,128]{2,1,0:T(8,128)(2,1)S(1)} %all-to-all-done.2.got_ref, bf16[2,896,512]{2,1,0:T(8,128)(2,1)S(1)} %factor.1.factor_ref, f32[128,128]{1,0:T(8,128)S(1)} %copy-done, f32[2,64,512]{2,1,0:T(8,128)S(1)} %get-tuple-element.22.diagonal_ref), custom_call_target="tpu_custom_call" | custom-call | flops 1000000000 | bytes 3000000 | tf_op jit(solution)/shard_map/final/pallas_call | solution.py:430
Async XLA Ops:
  1.7 10.5 %collective-permute-start = (bf16[80,512]{1,0:T(8,128)(2,1)S(1)}, bf16[80,512]{1,0:T(8,128)(2,1)S(1)}, u32[]{:S(2)}, u32[]{:S(2)}) collective-permute-start(bf16[80,512]{1,0:T(8,128)(2,1)S(1)} %get-tuple-element.14.own_ref), channel_id=1, source_target_pairs={{0,1},{1,0},{2,3},{3,2},{4,5},{5,4},{6,7},{7,6},{8,9},{9,8},{10,11... | collective-permute-start | bytes 245768 | tf_op jit(solution)/shard_map/ppermute | solution.py:323
  22.8 39.3 %all-to-all-start.1 = ((s16[32,16,128]{2,1,0:T(8,128)(2,1)}), s16[32,16,128]{2,1,0:T(8,128)(2,1)S(1)}, u32[]{:S(2)}, u32[]{:S(2)}) async-start(s16[32,16,128]{2,1,0:T(8,128)(2,1)} %line.1), calls=%async_computation.1 | async-start | bytes 262144 | tf_op jit(solution)/shard_map/all_to_all | solution.py:327
  37.2 18.0 %collective-permute-start.1 = (bf16[80,512]{1,0:T(8,128)(2,1)S(1)}, bf16[80,512]{1,0:T(8,128)(2,1)S(1)}, u32[]{:S(2)}, u32[]{:S(2)}) collective-permute-start(bf16[80,512]{1,0:T(8,128)(2,1)S(1)} %get-tuple-element.14.own_ref), channel_id=1, source_target_pairs={{0,2},{2,0},{1,3},{3,1},{4,6},{6,4},{5,7},{7,5},{8,10},{10,8},{9,1... | collective-permute-start | bytes 245768 | tf_op jit(solution)/shard_map/ppermute | solution.py:323
  55.2 5.8 %collective-permute-start.2 = (bf16[80,512]{1,0:T(8,128)(2,1)S(1)}, bf16[80,512]{1,0:T(8,128)(2,1)S(1)}, u32[]{:S(2)}, u32[]{:S(2)}) collective-permute-start(bf16[80,512]{1,0:T(8,128)(2,1)S(1)} %collective-permute-done.1.far_ref), channel_id=1, source_target_pairs={{0,1},{1,0},{2,3},{3,2},{4,5},{5,4},{6,7},{7,6},{8,9},{9,8},{10,11... | collective-permute-start | bytes 245768 | tf_op jit(solution)/shard_map/ppermute | solution.py:323
  63.0 12.0 %all-to-all-start.2 = ((s16[8,144,128]{2,1,0:T(8,128)(2,1)}), s16[8,144,128]{2,1,0:T(8,128)(2,1)S(1)}, u32[]{:S(2)}, u32[]{:S(2)}) async-start(s16[8,144,128]{2,1,0:T(8,128)(2,1)} %depth.1), calls=%async_computation.2 | async-start | bytes 589824 | tf_op jit(solution)/shard_map/all_to_all | solution.py:327
  68.2 6.8 %copy-start = (f32[128,128]{1,0:T(8,128)S(1)}, f32[128,128]{1,0:T(8,128)}, u32[]{:S(2)}) copy-start(f32[128,128]{1,0:T(8,128)} %coupling_ref.1) | copy-start | bytes 196612
where the time goes:
time: 77.2 us; the launch traced here: 76.8 us
  starting transfers between devices  44.9 us (58%)
  waiting for transfers between devices  12.3 us (16%)
  Pallas kernels  10.7 us (14%)
  blocking collectives  8.03 us (10%)
    ppermute x3, starting transfers between devices, swap(): return lax.ppermute(value, axis, [(0, 1), (1, 0)])  25.4 us
    all_to_all x2, starting transfers between devices, exchange(): return lax.all_to_all(value, axes, 0, 0, tiled=True)  19.5 us
    all_to_all x1, blocking collectives, exchange(): return lax.all_to_all(value, axes, 0, 0, tiled=True)  8.03 us
    ppermute x3, waiting for transfers between devices, swap(): return lax.ppermute(value, axis, [(0, 1), (1, 0)])  6.18 us
    all_to_all x2, waiting for transfers between devices, exchange(): return lax.all_to_all(value, axes, 0, 0, tiled=True)  6.15 us
    pallas_call x1, Pallas kernels, on_device(): pl.pallas_call(near_kernel, out_shape=(jax.ShapeDtypeStruct((2, PROBES, K...  1.83 us
    pallas_call x1, Pallas kernels, on_device(): pl.pallas_call(final_kernel, out_shape=jax.ShapeDtypeStruct((2, PROBES, W...  1.78 us
    pallas_call x1, Pallas kernels, on_device(): pl.pallas_call(own_kernel, out_shape=(jax.ShapeDtypeStruct((2, PROBES, LA...  1.7 us
  transfers between devices with their start and end apart: 5, of which 2 were waited for; matrix products, arithmetic and copies ran while one was open for 0% of the time, Pallas kernels for 6%

commit v1 on v0

--- a/solution.py
+++ b/solution.py
@@ -18,9 +18,9 @@
 TRANSFER = 80
 LANES = 1024
 BLOCK = 256
-KEPT = WIDTH + RANK
+PASSED = TRANSFER + 32
 ALL_SPANS = ((0, 256), (256, 512), (512, 768), (768, 1024))
-LATE_SPANS = ((0, 256), (256, 512), (512, 640))
+LATE_SPANS = ((0, 256), (256, 512))
 ROOT = math.sqrt(math.log2(math.e))
 TWO_LN2 = 2.0 * math.log(2.0)
 F32 = jnp.float32
@@ -183,17 +183,22 @@
 
 
 def near_kernel(other_ref, facts_ref, held_ref, right_ref, kept_ref, line_ref, sums):
+    y = lax.axis_index("y")
     zl = lax.axis_index("zl")
     sums[...] = held_ref[...]
     accumulate(other_ref, facts_ref, right_ref, sums, ALL_SPANS, False)
-    kept_ref[...] = sums[:, :, :KEPT]
-    units = [unit_of(sums, level) for level in range(2, LEVELS)]
+    kept_ref[...] = sums[:, :, :WIDTH]
+    units = [unit_of(sums, level) for level in range(LEVELS)]
     blank = jnp.zeros((QUARTER, 128), I16)
+    whole = jnp.zeros((PROBES, 128), I16)
     for at in range(4):
         part = slice(at * QUARTER, (at + 1) * QUARTER)
-        higher = [unit[part] for unit in units[1:]]
-        line_ref[zl * 4 + at] = jnp.concatenate([blank] + higher, axis=0)
-        line_ref[(1 - zl) * 4 + at] = jnp.concatenate([units[0][part]] + higher, axis=0)
+        higher = [unit[part] for unit in units[3:]]
+        line_ref[zl * 4 + at, 0 : 5 * QUARTER] = jnp.concatenate([blank] + higher, axis=0)
+        line_ref[(1 - zl) * 4 + at, 0 : 5 * QUARTER] = jnp.concatenate([units[2][part]] + higher, axis=0)
+        line_ref[(1 - zl) * 4 + at, 5 * QUARTER :] = whole
+    for apart, unit in ((0, whole), (1, units[0]), (2, units[1]), (3, units[1])):
+        line_ref[zl * 4 + jnp.bitwise_xor(y, apart), 5 * QUARTER :] = unit
 
 
 def added(parts):
@@ -202,12 +207,13 @@
     return parts[0]
 
 
-def line_kernel(got_ref, out_ref):
+def line_kernel(got_ref, message_ref, out_ref, passed_ref):
     x = lax.axis_index("x")
+    y = lax.axis_index("y")
     zh = lax.axis_index("zh")
     zl = lax.axis_index("zl")
     two = encode(added([decode(got_ref[(1 - zl) * 4 + at, 0:QUARTER]) for at in range(4)]))
-    packed = encode(added([decode(got_ref[at, QUARTER:]) for at in range(8)]))
+    packed = encode(added([decode(got_ref[at, QUARTER : 5 * QUARTER]) for at in range(8)]))
     parts = [packed[at * QUARTER : (at + 1) * QUARTER] for at in range(4)]
     for aside in range(4):
         for apart in range(4):
@@ -220,25 +226,27 @@
                 piece = two
             for half in range(2):
                 out_ref[place + half] = piece
-
-
-def far_kernel(far_ref, facts_ref, kept_ref, right_ref, out_ref):
+    passed_ref[0:TRANSFER, :] = message_ref[...]
+    first, second, third = [
+        decode(got_ref[zl * 4 + jnp.bitwise_xor(y, apart), 5 * QUARTER :]) for apart in (1, 2, 3)
+    ]
+    low = jnp.concatenate([first, second + third], axis=0).astype(BF16)
+    for at in range(4):
+        passed_ref[TRANSFER:, at * 128 : (at + 1) * 128] = low[at * 32 : (at + 1) * 32]
+
+
+def relay_kernel(far_ref, own_ref, out_ref):
+    out_ref[0:TRANSFER, :] = far_ref[0:TRANSFER, :]
+    total = far_ref[TRANSFER:, :].astype(F32) + own_ref[TRANSFER:, :].astype(F32)
+    out_ref[TRANSFER:, :] = total.astype(BF16)
+
+
+def late_kernel(far_ref, facts_ref, kept_ref, right_ref, out_ref):
     out_ref[...] = kept_ref[...]
     accumulate(far_ref, facts_ref, right_ref, out_ref, LATE_SPANS, False)
 
 
-def cross_kernel(cross_ref, facts_ref, kept_ref, right_ref, diagonal_ref, low_ref, sums):
-    y = lax.axis_index("y")
-    sums[...] = kept_ref[...]
-    accumulate(cross_ref, facts_ref, right_ref, sums, LATE_SPANS, False)
-    diagonal_ref[...] = sums[:, :, :WIDTH]
-    units = [unit_of(sums, level) for level in range(2)]
-    low_ref[y] = jnp.zeros((PROBES, 128), I16)
-    for apart, level in ((1, 0), (2, 1), (3, 1)):
-        low_ref[jnp.bitwise_xor(y, apart)] = units[level]
-
-
-def depth_kernel(got_ref, low_ref, out_ref):
+def depth_kernel(got_ref, out_ref):
     x = lax.axis_index("x")
     zh = lax.axis_index("zh")
 
@@ -256,25 +264,22 @@
         total((2, 3), range(4)),
     ]
     packed = encode(jnp.concatenate(found, axis=0))
-    for at in range(4):
-        for core in range(2):
-            out_ref[2 * at + core, 0:PROBES] = low_ref[at]
-            out_ref[2 * at + core, PROBES:] = packed
-
-
-def final_kernel(got_ref, factor_ref, coupling_ref, diagonal_ref, out_ref, sibling):
-    y = lax.axis_index("y")
+    for place in range(8):
+        out_ref[place] = packed
+
+
+def final_kernel(got_ref, factor_ref, coupling_ref, diagonal_ref, relay_ref, cross_ref, out_ref, sibling):
     row = row_index()
+    mine = lax.axis_index("c")
     for core in range(2):
         lanes = slice(core * 128, core * 128 + 128)
-        sibling[0:PROBES, lanes] = decode(got_ref[jnp.bitwise_xor(y, 1) * 2 + core, 0:PROBES])
-        pair = decode(got_ref[jnp.bitwise_xor(y, 2) * 2 + core, 0:PROBES])
-        pair = pair + decode(got_ref[jnp.bitwise_xor(y, 3) * 2 + core, 0:PROBES])
-        sibling[PROBES : 2 * PROBES, lanes] = pair
+        for at in range(4):
+            parts = [ref[TRANSFER:, at * 128 : (at + 1) * 128].astype(F32) for ref in (relay_ref, cross_ref)]
+            sibling[at * 32 : (at + 1) * 32, lanes] = jnp.where(mine == core, parts[0], parts[1])
         for level in range(2, LEVELS):
             for at in range(4):
                 start = level * PROBES + at * QUARTER
-                source = PROBES + (level - 2) * QUARTER
+                source = (level - 2) * QUARTER
                 sibling[start : start + QUARTER, lanes] = decode(got_ref[2 * at + core, source : source + QUARTER])
     coupling = coupling_ref[...]
     blank = jnp.zeros((HALF, RANK), F32)
@@ -364,8 +369,8 @@
     kept, line = pl.pallas_call(
         near_kernel,
         out_shape=(
-            jax.ShapeDtypeStruct((2, PROBES, KEPT), F32),
-            jax.ShapeDtypeStruct((8, 5 * QUARTER, 128), I16),
+            jax.ShapeDtypeStruct((2, PROBES, WIDTH), F32),
+            jax.ShapeDtypeStruct((8, 5 * QUARTER + PROBES, 128), I16),
         ),
         in_specs=[VMEM] * 4,
         out_specs=(VMEM, VMEM),
@@ -375,39 +380,20 @@
         name="near",
     )(other, facts, held, right)
     line = exchange(line, ("zl", "y"))
-    deep = pl.pallas_call(
+    deep, passed = pl.pallas_call(
         line_kernel,
-        out_shape=jax.ShapeDtypeStruct((32, QUARTER, 128), I16),
-        in_specs=[VMEM],
-        out_specs=VMEM,
+        out_shape=(
+            jax.ShapeDtypeStruct((32, QUARTER, 128), I16),
+            jax.ShapeDtypeStruct((PASSED, WIDTH), BF16),
+        ),
+        in_specs=[VMEM] * 2,
+        out_specs=(VMEM, VMEM),
         compiler_params=ROOM,
         cost_estimate=cost(10**5, 3 * 10**5),
         name="line",
-    )(line)
+    )(line, message)
     deep = exchange(deep, ("x", "zh", "h"))
-    cross = swap(far, "c")
-    kept = pl.pallas_call(
-        far_kernel,
-        out_shape=jax.ShapeDtypeStruct((2, PROBES, KEPT), F32),
-        in_specs=[VMEM] * 4,
-        out_specs=VMEM,
-        compiler_params=ROOM,
-        cost_estimate=cost(10**9, 2 * 10**6),
-        name="far",
-    )(far, facts, kept, right)
-    diagonal, low = pl.pallas_call(
-        cross_kernel,
-        out_shape=(
-            jax.ShapeDtypeStruct((2, PROBES, WIDTH), F32),
-            jax.ShapeDtypeStruct((4, PROBES, 128), I16),
-        ),
-        in_specs=[VMEM] * 4,
-        out_specs=(VMEM, VMEM),
-        scratch_shapes=[pltpu.VMEM((2, PROBES, KEPT), F32)],
-        compiler_params=ROOM,
-        cost_estimate=cost(10**9, 2 * 10**6),
-        name="cross",
-    )(cross, facts, kept, right)
+    far = swap(passed, "h")
     factor = pl.pallas_call(
         factor_kernel,
         out_shape=jax.ShapeDtypeStruct((2, LEVELS * RANK, WIDTH), BF16),
@@ -419,24 +405,47 @@
     )(facts, marks, right)
     wide = pl.pallas_call(
         depth_kernel,
-        out_shape=jax.ShapeDtypeStruct((8, PROBES + 5 * QUARTER, 128), I16),
+        out_shape=jax.ShapeDtypeStruct((8, 5 * QUARTER, 128), I16),
+        in_specs=[VMEM],
+        out_specs=VMEM,
+        compiler_params=ROOM,
+        cost_estimate=cost(10**5, 5 * 10**5),
+        name="depth",
+    )(deep)
+    wide = exchange(wide, ("y", "c"))
+    relay = pl.pallas_call(
+        relay_kernel,
+        out_shape=jax.ShapeDtypeStruct((PASSED, WIDTH), BF16),
         in_specs=[VMEM] * 2,
         out_specs=VMEM,
         compiler_params=ROOM,
         cost_estimate=cost(10**5, 5 * 10**5),
-        name="depth",
-    )(deep, low)
-    wide = exchange(wide, ("y", "c"))
+        name="relay",
+    )(far, passed)
+    cross = swap(relay, "c")
+
+    def late(points, sums):
+        return pl.pallas_call(
+            late_kernel,
+            out_shape=jax.ShapeDtypeStruct((2, PROBES, WIDTH), F32),
+            in_specs=[VMEM] * 4,
+            out_specs=VMEM,
+            compiler_params=ROOM,
+            cost_estimate=cost(10**9, 2 * 10**6),
+        )(points, facts, sums, right)
+
+    kept = late(relay, kept)
+    diagonal = late(cross, kept)
     return pl.pallas_call(
         final_kernel,
         out_shape=jax.ShapeDtypeStruct((2, PROBES, WIDTH), F32),
-        in_specs=[VMEM] * 4,
+        in_specs=[VMEM] * 6,
         out_specs=VMEM,
         scratch_shapes=[pltpu.VMEM((LEVELS * PROBES, 2 * RANK), F32)],
         compiler_params=ROOM,
         cost_estimate=cost(10**9, 3 * 10**6),
         name="final",
-    )(wide, factor, coupling, diagonal)
+    )(wide, factor, coupling, diagonal, relay, cross)
 
 
 def solution(mesh):

time: 77.2 us -> 78.9 us (1.022)
  waiting for transfers between devices: 12.3 us -> 16.3 us
  starting transfers between devices: 44.9 us -> 41.3 us
  blocking collectives: 8.03 us -> 9.99 us
    ppermute x3, waiting for transfers between devices: 6.18 us -> 12.3 us  [swap(): return lax.ppermute(value, axis, [(0, 1), (1, 0)])]
    all_to_all x2, waiting for transfers between devices: 6.15 us -> 4.03 us  [exchange(): return lax.all_to_all(value, axes, 0, 0, tiled=True)]
    all_to_all x1, blocking collectives: 8.03 us -> 9.99 us  [exchange(): return lax.all_to_all(value, axes, 0, 0, tiled=True)]
    all_to_all x2, starting transfers between devices: 19.5 us -> 17.6 us  [exchange(): return lax.all_to_all(value, axes, 0, 0, tiled=True)]
    ppermute x3, starting transfers between devices: 25.4 us -> 23.7 us  [swap(): return lax.ppermute(value, axis, [(0, 1), (1, 0)])]
    pallas_call x5 -> x6, Pallas kernels: 5.61 us -> 4.95 us  [the longest x1 1.84 us: on_device(): pl.pallas_call(near_kernel, out_shape=(jax.ShapeDtypeStruct((2, PROBES, W...]
where the time goes in v1:
time: 78.9 us; the launch traced here: 78.5 us
  starting transfers between devices  41.3 us (52%)
  waiting for transfers between devices  16.3 us (21%)
  Pallas kernels  10.1 us (13%)
  blocking collectives  9.99 us (13%)
    ppermute x3, starting transfers between devices, swap(): return lax.ppermute(value, axis, [(0, 1), (1, 0)])  23.7 us
    all_to_all x2, starting transfers between devices, exchange(): return lax.all_to_all(value, axes, 0, 0, tiled=True)  17.6 us
    ppermute x3, waiting for transfers between devices, swap(): return lax.ppermute(value, axis, [(0, 1), (1, 0)])  12.3 us
    all_to_all x1, blocking collectives, exchange(): return lax.all_to_all(value, axes, 0, 0, tiled=True)  9.99 us
    all_to_all x2, waiting for transfers between devices, exchange(): return lax.all_to_all(value, axes, 0, 0, tiled=True)  4.03 us
    pallas_call x1, Pallas kernels, on_device(): pl.pallas_call(near_kernel, out_shape=(jax.ShapeDtypeStruct((2, PROBES, W...  1.84 us
    pallas_call x1, Pallas kernels, on_device(): pl.pallas_call(final_kernel, out_shape=jax.ShapeDtypeStruct((2, PROBES, W...  1.78 us
    pallas_call x1, Pallas kernels, on_device(): pl.pallas_call(own_kernel, out_shape=(jax.ShapeDtypeStruct((2, PROBES, LA...  1.7 us
  transfers between devices with their start and end apart: 5, of which 2 were waited for; matrix products, arithmetic and copies ran while one was open for 0% of the time, Pallas kernels for 6%

profile of v1, /device:TPU:1, one launch (start us, length us, event | category | flops | bytes accessed | tf_op | source)
XLA Modules:
  0.0 78.5 jit_solution(408924428225360798)
XLA Ops:
  0.7 1.0 %prepare.1 = (bf16[80,512]{1,0:T(8,128)(2,1)S(1)}, f32[7,8,128]{2,1,0:T(8,128)S(1)}, f32[16,128]{1,0:T(8,128)S(1)}) custom-call(s32[8,512]{1,0:T(8,128)} %coords_ref.1, f32[64,512]{1,0:T(8,128)} %probes_ref.1, f32[254,8,128]{2,1,0:T(8,128)} %marks_ref.1, f32[8]{0:T(128)} %scales_ref.1, f32[1]{0:T(128)S(6)} %copy.7.strength_ref), custom_call_target="tpu_custom_call" | custom-call | flops 100000 | bytes 200000 | tf_op jit(solution)/shard_map/prepare/pallas_call | solution.py:336
  1.7 8.7 %collective-permute-start = (bf16[80,512]{1,0:T(8,128)(2,1)S(1)}, bf16[80,512]{1,0:T(8,128)(2,1)S(1)}, u32[]{:S(2)}, u32[]{:S(2)}) collective-permute-start(bf16[80,512]{1,0:T(8,128)(2,1)S(1)} %get-tuple-element.14.own_ref.message_ref), channel_id=1, source_target_pairs={{0,1},{1,0},{2,3},{3,2},{4,5},{5,4},{6,7},{7,6},{8,9},{9,8},{10,11... | collective-permute-start | bytes 245768 | tf_op jit(solution)/shard_map/ppermute | solution.py:328
  10.4 1.7 %own.1 = (f32[2,64,1024]{2,1,0:T(8,128)S(1)}, bf16[128,1024]{1,0:T(8,128)(2,1)S(1)}) custom-call(bf16[80,512]{1,0:T(8,128)(2,1)S(1)} %get-tuple-element.14.own_ref.message_ref, f32[16,128]{1,0:T(8,128)S(1)} %get-tuple-element.15.facts_ref, f32[7,8,128]{2,1,0:T(8,128)S(1)} %get-tuple-element.16.marks_ref), custom_call_target="tpu_custom_call" | custom-call | flops 1000000000 | bytes 2000000 | tf_op jit(solution)/shard_map/own/pallas_call | solution.py:357
  12.2 0.0 collective-permute-done.other_ref
  12.2 1.8 %near.1 = (f32[2,64,512]{2,1,0:T(8,128)S(1)}, s16[8,144,128]{2,1,0:T(8,128)(2,1)S(1)}) custom-call(bf16[80,512]{1,0:T(8,128)(2,1)S(1)} %collective-permute-done.other_ref, f32[16,128]{1,0:T(8,128)S(1)} %get-tuple-element.15.facts_ref, f32[2,64,1024]{2,1,0:T(8,128)S(1)} %get-tuple-element.17.held_ref, bf16[128,1024]{1,0:T(8,128)(2,1)S(1)} %get-tuple-element.18.right_ref), custom_call_target="tpu_custom_call" | custom-call | flops 1000000000 | bytes 2000000 | tf_op jit(solution)/shard_map/near/pallas_call | solution.py:369
  14.0 10.0 %all_to_all.15.got_ref = s16[8,144,128]{2,1,0:T(8,128)(2,1)S(1)} all-to-all(s16[8,144,128]{2,1,0:T(8,128)(2,1)S(1)} %get-tuple-element.19), channel_id=1, replica_groups=mesh['x'=4,'zh'=4,'zl'=2,'y'=4,'h'=2,'c'=2] {'zl','y'}, dimensions={0} | all-to-all | bytes 589824 | tf_op jit(solution)/shard_map/all_to_all | solution.py:332
  24.0 0.8 %line.1 = (s16[32,16,128]{2,1,0:T(8,128)(2,1)}, bf16[112,512]{1,0:T(8,128)(2,1)S(1)}) custom-call(s16[8,144,128]{2,1,0:T(8,128)(2,1)S(1)} %all_to_all.15.got_ref, bf16[80,512]{1,0:T(8,128)(2,1)S(1)} %get-tuple-element.14.own_ref.message_ref), custom_call_target="tpu_custom_call" | custom-call | flops 100000 | bytes 300000 | tf_op jit(solution)/shard_map/line/pallas_call | solution.py:383
  24.8 14.2 %all-to-all-start.1 = ((s16[32,16,128]{2,1,0:T(8,128)(2,1)}), s16[32,16,128]{2,1,0:T(8,128)(2,1)S(1)}, u32[]{:S(2)}, u32[]{:S(2)}) async-start(s16[32,16,128]{2,1,0:T(8,128)(2,1)} %get-tuple-element.20), calls=%async_computation.1 | async-start | bytes 262144 | tf_op jit(solution)/shard_map/all_to_all | solution.py:332
  39.1 11.9 %collective-permute-start.1 = (bf16[112,512]{1,0:T(8,128)(2,1)S(1)}, bf16[112,512]{1,0:T(8,128)(2,1)S(1)}, u32[]{:S(2)}, u32[]{:S(2)}) collective-permute-start(bf16[112,512]{1,0:T(8,128)(2,1)S(1)} %get-tuple-element.21.own_ref), channel_id=1, source_target_pairs={{0,2},{2,0},{1,3},{3,1},{4,6},{6,4},{5,7},{7,5},{8,10},{10,8},{9,1... | collective-permute-start | bytes 344072 | tf_op jit(solution)/shard_map/ppermute | solution.py:328
  50.9 12.3 %collective-permute-done.1.far_ref = bf16[112,512]{1,0:T(8,128)(2,1)S(1)} collective-permute-done((bf16[112,512]{1,0:T(8,128)(2,1)S(1)}, bf16[112,512]{1,0:T(8,128)(2,1)S(1)}, u32[]{:S(2)}, u32[]{:S(2)}) %collective-permute-start.1) | collective-permute-done | bytes 114720 | tf_op jit(solution)/shard_map/ppermute | solution.py:328
  63.2 3.1 %collective-permute-start.2 = (bf16[112,512]{1,0:T(8,128)(2,1)S(1)}, bf16[112,512]{1,0:T(8,128)(2,1)S(1)}, u32[]{:S(2)}, u32[]{:S(2)}) collective-permute-start(bf16[112,512]{1,0:T(8,128)(2,1)S(1)} %relay.1.far_ref.relay_ref), channel_id=1, source_target_pairs={{0,1},{1,0},{2,3},{3,2},{4,5},{5,4},{6,7},{7,6},{8,9},{9,8},{10,11... | collective-permute-start | bytes 344072 | tf_op jit(solution)/shard_map/ppermute | solution.py:328
  66.3 0.6 factor.1.factor_ref
  67.0 0.0 all-to-all-done.1.got_ref
  67.0 0.8 %depth.1 = s16[8,80,128]{2,1,0:T(8,128)(2,1)} custom-call(s16[32,16,128]{2,1,0:T(8,128)(2,1)S(1)} %all-to-all-done.1.got_ref), custom_call_target="tpu_custom_call" | custom-call | flops 100000 | bytes 500000 | tf_op jit(solution)/shard_map/depth/pallas_call | solution.py:406
  67.8 3.3 %all-to-all-start.2 = ((s16[8,80,128]{2,1,0:T(8,128)(2,1)}), s16[8,80,128]{2,1,0:T(8,128)(2,1)S(1)}, u32[]{:S(2)}, u32[]{:S(2)}) async-start(s16[8,80,128]{2,1,0:T(8,128)(2,1)} %depth.1), calls=%async_computation.2 | async-start | bytes 327680 | tf_op jit(solution)/shard_map/all_to_all | solution.py:332
  71.1 0.7 shard_map.64.kept_ref
  71.9 0.0 copy-start
  71.9 0.0 collective-permute-done.2.far_ref.cross_ref
  71.9 0.7 shard_map.65.diagonal_ref
  72.7 4.0 %all-to-all-done.2.got_ref = s16[8,80,128]{2,1,0:T(8,128)(2,1)S(1)} async-done(((s16[8,80,128]{2,1,0:T(8,128)(2,1)}), s16[8,80,128]{2,1,0:T(8,128)(2,1)S(1)}, u32[]{:S(2)}, u32[]{:S(2)}) %all-to-all-start.2) | async-done | bytes 163872 | tf_op jit(solution)/shard_map/all_to_all | solution.py:332
  76.7 0.0 copy-done
  76.7 1.8 %final.1 = f32[2,64,512]{2,1,0:T(8,128)} custom-call(s16[8,80,128]{2,1,0:T(8,128)(2,1)S(1)} %all-to-all-done.2.got_ref, bf16[2,896,512]{2,1,0:T(8,128)(2,1)S(1)} %factor.1.factor_ref, f32[128,128]{1,0:T(8,128)S(1)} %copy-done, f32[2,64,512]{2,1,0:T(8,128)S(1)} %shard_map.65.diagonal_ref, bf16[112,512]{1,0:T(8,128)(2,1)S(1)} %relay.1.far_ref.relay_ref, ...), custom_call_target="tpu_custom_call" | custom-call | flops 1000000000 | bytes 3000000 | tf_op jit(solution)/shard_map/final/pallas_call | solution.py:439
  (1 shorter events, 0.0 us)
Async XLA Ops:
  1.7 10.5 %collective-permute-start = (bf16[80,512]{1,0:T(8,128)(2,1)S(1)}, bf16[80,512]{1,0:T(8,128)(2,1)S(1)}, u32[]{:S(2)}, u32[]{:S(2)}) collective-permute-start(bf16[80,512]{1,0:T(8,128)(2,1)S(1)} %get-tuple-element.14.own_ref.message_ref), channel_id=1, source_target_pairs={{0,1},{1,0},{2,3},{3,2},{4,5},{5,4},{6,7},{7,6},{8,9},{9,8},{10,11... | collective-permute-start | bytes 245768 | tf_op jit(solution)/shard_map/ppermute | solution.py:328
  24.8 42.2 %all-to-all-start.1 = ((s16[32,16,128]{2,1,0:T(8,128)(2,1)}), s16[32,16,128]{2,1,0:T(8,128)(2,1)S(1)}, u32[]{:S(2)}, u32[]{:S(2)}) async-start(s16[32,16,128]{2,1,0:T(8,128)(2,1)} %get-tuple-element.20), calls=%async_computation.1 | async-start | bytes 262144 | tf_op jit(solution)/shard_map/all_to_all | solution.py:332
  39.1 24.1 %collective-permute-start.1 = (bf16[112,512]{1,0:T(8,128)(2,1)S(1)}, bf16[112,512]{1,0:T(8,128)(2,1)S(1)}, u32[]{:S(2)}, u32[]{:S(2)}) collective-permute-start(bf16[112,512]{1,0:T(8,128)(2,1)S(1)} %get-tuple-element.21.own_ref), channel_id=1, source_target_pairs={{0,2},{2,0},{1,3},{3,1},{4,6},{6,4},{5,7},{7,5},{8,10},{10,8},{9,1... | collective-permute-start | bytes 344072 | tf_op jit(solution)/shard_map/ppermute | solution.py:328
  63.2 8.7 %collective-permute-start.2 = (bf16[112,512]{1,0:T(8,128)(2,1)S(1)}, bf16[112,512]{1,0:T(8,128)(2,1)S(1)}, u32[]{:S(2)}, u32[]{:S(2)}) collective-permute-start(bf16[112,512]{1,0:T(8,128)(2,1)S(1)} %relay.1.far_ref.relay_ref), channel_id=1, source_target_pairs={{0,1},{1,0},{2,3},{3,2},{4,5},{5,4},{6,7},{7,6},{8,9},{9,8},{10,11... | collective-permute-start | bytes 344072 | tf_op jit(solution)/shard_map/ppermute | solution.py:328
  67.8 8.9 %all-to-all-start.2 = ((s16[8,80,128]{2,1,0:T(8,128)(2,1)}), s16[8,80,128]{2,1,0:T(8,128)(2,1)S(1)}, u32[]{:S(2)}, u32[]{:S(2)}) async-start(s16[8,80,128]{2,1,0:T(8,128)(2,1)} %depth.1), calls=%async_computation.2 | async-start | bytes 327680 | tf_op jit(solution)/shard_map/all_to_all | solution.py:332
  71.9 4.8 %copy-start = (f32[128,128]{1,0:T(8,128)S(1)}, f32[128,128]{1,0:T(8,128)}, u32[]{:S(2)}) copy-start(f32[128,128]{1,0:T(8,128)} %coupling_ref.1) | copy-start | bytes 196612

commit v2 on v0

--- a/solution.py
+++ b/solution.py
@@ -19,7 +19,8 @@
 LANES = 1024
 BLOCK = 256
 KEPT = WIDTH + RANK
-ALL_SPANS = ((0, 256), (256, 512), (512, 768), (768, 1024))
+NEAR_SPANS = ((512, 768), (768, 1024))
+SELF_SPANS = ((0, 256), (256, 512))
 LATE_SPANS = ((0, 256), (256, 512), (512, 640))
 ROOT = math.sqrt(math.log2(math.e))
 TWO_LN2 = 2.0 * math.log(2.0)
@@ -169,7 +170,7 @@
     halves.append(jnp.zeros((8, HALF), F32))
     columns = jnp.concatenate([own] + halves, axis=1)
     right_ref[...] = right_form(columns, facts_ref[8:9, 0:1]).astype(BF16)
-    accumulate(own_ref, facts_ref, right_ref, held_ref, ALL_SPANS, True)
+    accumulate(own_ref, facts_ref, right_ref, held_ref, NEAR_SPANS, True)
 
 
 def factor_kernel(facts_ref, marks_ref, right_ref, factor_ref):
@@ -184,9 +185,9 @@
 
 def near_kernel(other_ref, facts_ref, held_ref, right_ref, kept_ref, line_ref, sums):
     zl = lax.axis_index("zl")
-    sums[...] = held_ref[...]
-    accumulate(other_ref, facts_ref, right_ref, sums, ALL_SPANS, False)
-    kept_ref[...] = sums[:, :, :KEPT]
+    sums[:, :, WIDTH:] = held_ref[:, :, WIDTH:]
+    accumulate(other_ref, facts_ref, right_ref, sums, NEAR_SPANS, False)
+    kept_ref[...] = sums[:, :, WIDTH:KEPT]
     units = [unit_of(sums, level) for level in range(2, LEVELS)]
     blank = jnp.zeros((QUARTER, 128), I16)
     for at in range(4):
@@ -222,8 +223,10 @@
                 out_ref[place + half] = piece
 
 
-def far_kernel(far_ref, facts_ref, kept_ref, right_ref, out_ref):
-    out_ref[...] = kept_ref[...]
+def far_kernel(far_ref, own_ref, other_ref, facts_ref, kept_ref, right_ref, out_ref):
+    out_ref[:, :, WIDTH:] = kept_ref[...]
+    accumulate(own_ref, facts_ref, right_ref, out_ref, SELF_SPANS, True)
+    accumulate(other_ref, facts_ref, right_ref, out_ref, SELF_SPANS, False)
     accumulate(far_ref, facts_ref, right_ref, out_ref, LATE_SPANS, False)
 
 
@@ -364,7 +367,7 @@
     kept, line = pl.pallas_call(
         near_kernel,
         out_shape=(
-            jax.ShapeDtypeStruct((2, PROBES, KEPT), F32),
+            jax.ShapeDtypeStruct((2, PROBES, RANK), F32),
             jax.ShapeDtypeStruct((8, 5 * QUARTER, 128), I16),
         ),
         in_specs=[VMEM] * 4,
@@ -389,12 +392,12 @@
     kept = pl.pallas_call(
         far_kernel,
         out_shape=jax.ShapeDtypeStruct((2, PROBES, KEPT), F32),
-        in_specs=[VMEM] * 4,
+        in_specs=[VMEM] * 6,
         out_specs=VMEM,
         compiler_params=ROOM,
         cost_estimate=cost(10**9, 2 * 10**6),
         name="far",
-    )(far, facts, kept, right)
+    )(far, message, other, facts, kept, right)
     diagonal, low = pl.pallas_call(
         cross_kernel,
         out_shape=(

time: 77.2 us -> 77.2 us (level)
  no operation moved by 1% of the time
where the time goes in v2:
time: 77.2 us; the launch traced here: 76.8 us
  starting transfers between devices  44.9 us (58%)
  waiting for transfers between devices  12.3 us (16%)
  Pallas kernels  10.8 us (14%)
  blocking collectives  8.03 us (10%)
    ppermute x3, starting transfers between devices, swap(): return lax.ppermute(value, axis, [(0, 1), (1, 0)])  25.4 us
    all_to_all x2, starting transfers between devices, exchange(): return lax.all_to_all(value, axes, 0, 0, tiled=True)  19.5 us
    all_to_all x1, blocking collectives, exchange(): return lax.all_to_all(value, axes, 0, 0, tiled=True)  8.03 us
    ppermute x3, waiting for transfers between devices, swap(): return lax.ppermute(value, axis, [(0, 1), (1, 0)])  6.18 us
    all_to_all x2, waiting for transfers between devices, exchange(): return lax.all_to_all(value, axes, 0, 0, tiled=True)  6.15 us
    pallas_call x1, Pallas kernels, on_device(): pl.pallas_call(final_kernel, out_shape=jax.ShapeDtypeStruct((2, PROBES, W...  1.78 us
    pallas_call x1, Pallas kernels, on_device(): pl.pallas_call(far_kernel, out_shape=jax.ShapeDtypeStruct((2, PROBES, KEP...  1.67 us
  transfers between devices with their start and end apart: 5, of which 2 were waited for; matrix products, arithmetic and copies ran while one was open for 0% of the time, Pallas kernels for 6%

profile of v2, /device:TPU:1, one launch (start us, length us, event | category | flops | bytes accessed | tf_op | source)
XLA Modules:
  0.0 76.8 jit_solution(9305066025800277487)
XLA Ops:
  0.7 1.0 %prepare.1 = (bf16[80,512]{1,0:T(8,128)(2,1)S(1)}, f32[7,8,128]{2,1,0:T(8,128)S(1)}, f32[16,128]{1,0:T(8,128)S(1)}) custom-call(s32[8,512]{1,0:T(8,128)} %coords_ref.1, f32[64,512]{1,0:T(8,128)} %probes_ref.1, f32[254,8,128]{2,1,0:T(8,128)} %marks_ref.1, f32[8]{0:T(128)} %scales_ref.1, f32[1]{0:T(128)S(6)} %copy.7.strength_ref), custom_call_target="tpu_custom_call" | custom-call | flops 100000 | bytes 200000 | tf_op jit(solution)/shard_map/prepare/pallas_call | solution.py:334
  1.7 8.7 %collective-permute-start = (bf16[80,512]{1,0:T(8,128)(2,1)S(1)}, bf16[80,512]{1,0:T(8,128)(2,1)S(1)}, u32[]{:S(2)}, u32[]{:S(2)}) collective-permute-start(bf16[80,512]{1,0:T(8,128)(2,1)S(1)} %get-tuple-element.14.own_ref), channel_id=1, source_target_pairs={{0,1},{1,0},{2,3},{3,2},{4,5},{5,4},{6,7},{7,6},{8,9},{9,8},{10,11... | collective-permute-start | bytes 245768 | tf_op jit(solution)/shard_map/ppermute | solution.py:326
  10.4 1.4 %own.1 = (f32[2,64,1024]{2,1,0:T(8,128)S(1)}, bf16[128,1024]{1,0:T(8,128)(2,1)S(1)}) custom-call(bf16[80,512]{1,0:T(8,128)(2,1)S(1)} %get-tuple-element.14.own_ref, f32[16,128]{1,0:T(8,128)S(1)} %get-tuple-element.15.facts_ref, f32[7,8,128]{2,1,0:T(8,128)S(1)} %get-tuple-element.16.marks_ref), custom_call_target="tpu_custom_call" | custom-call | flops 1000000000 | bytes 2000000 | tf_op jit(solution)/shard_map/own/pallas_call | solution.py:355
  11.9 0.0 collective-permute-done.other_ref
  11.9 1.5 %near.1 = (f32[2,64,128]{2,1,0:T(8,128)S(1)}, s16[8,80,128]{2,1,0:T(8,128)(2,1)S(1)}) custom-call(bf16[80,512]{1,0:T(8,128)(2,1)S(1)} %collective-permute-done.other_ref, f32[16,128]{1,0:T(8,128)S(1)} %get-tuple-element.15.facts_ref, f32[2,64,1024]{2,1,0:T(8,128)S(1)} %get-tuple-element.17.held_ref, bf16[128,1024]{1,0:T(8,128)(2,1)S(1)} %get-tuple-element.18.right_ref), custom_call_target="tpu_custom_call" | custom-call | flops 1000000000 | bytes 2000000 | tf_op jit(solution)/shard_map/near/pallas_call | solution.py:367
  13.4 8.0 %all_to_all.15.got_ref = s16[8,80,128]{2,1,0:T(8,128)(2,1)S(1)} all-to-all(s16[8,80,128]{2,1,0:T(8,128)(2,1)S(1)} %get-tuple-element.19), channel_id=1, replica_groups=mesh['x'=4,'zh'=4,'zl'=2,'y'=4,'h'=2,'c'=2] {'zl','y'}, dimensions={0} | all-to-all | bytes 327680 | tf_op jit(solution)/shard_map/all_to_all | solution.py:330
  21.4 0.8 %line.1 = s16[32,16,128]{2,1,0:T(8,128)(2,1)} custom-call(s16[8,80,128]{2,1,0:T(8,128)(2,1)S(1)} %all_to_all.15.got_ref), custom_call_target="tpu_custom_call" | custom-call | flops 100000 | bytes 300000 | tf_op jit(solution)/shard_map/line/pallas_call | solution.py:381
  22.2 14.3 %all-to-all-start.1 = ((s16[32,16,128]{2,1,0:T(8,128)(2,1)}), s16[32,16,128]{2,1,0:T(8,128)(2,1)S(1)}, u32[]{:S(2)}, u32[]{:S(2)}) async-start(s16[32,16,128]{2,1,0:T(8,128)(2,1)} %line.1), calls=%async_computation.1 | async-start | bytes 262144 | tf_op jit(solution)/shard_map/all_to_all | solution.py:330
  36.6 11.9 %collective-permute-start.1 = (bf16[80,512]{1,0:T(8,128)(2,1)S(1)}, bf16[80,512]{1,0:T(8,128)(2,1)S(1)}, u32[]{:S(2)}, u32[]{:S(2)}) collective-permute-start(bf16[80,512]{1,0:T(8,128)(2,1)S(1)} %get-tuple-element.14.own_ref), channel_id=1, source_target_pairs={{0,2},{2,0},{1,3},{3,1},{4,6},{6,4},{5,7},{7,5},{8,10},{10,8},{9,1... | collective-permute-start | bytes 245768 | tf_op jit(solution)/shard_map/ppermute | solution.py:326
  48.5 6.2 %collective-permute-done.1.far_ref = bf16[80,512]{1,0:T(8,128)(2,1)S(1)} collective-permute-done((bf16[80,512]{1,0:T(8,128)(2,1)S(1)}, bf16[80,512]{1,0:T(8,128)(2,1)S(1)}, u32[]{:S(2)}, u32[]{:S(2)}) %collective-permute-start.1) | collective-permute-done | bytes 81952 | tf_op jit(solution)/shard_map/ppermute | solution.py:326
  54.6 4.8 %collective-permute-start.2 = (bf16[80,512]{1,0:T(8,128)(2,1)S(1)}, bf16[80,512]{1,0:T(8,128)(2,1)S(1)}, u32[]{:S(2)}, u32[]{:S(2)}) collective-permute-start(bf16[80,512]{1,0:T(8,128)(2,1)S(1)} %collective-permute-done.1.far_ref), channel_id=1, source_target_pairs={{0,1},{1,0},{2,3},{3,2},{4,5},{5,4},{6,7},{7,6},{8,9},{9,8},{10,11... | collective-permute-start | bytes 245768 | tf_op jit(solution)/shard_map/ppermute | solution.py:326
  59.4 1.7 %far.1.kept_ref = f32[2,64,640]{2,1,0:T(8,128)S(1)} custom-call(bf16[80,512]{1,0:T(8,128)(2,1)S(1)} %collective-permute-done.1.far_ref, bf16[80,512]{1,0:T(8,128)(2,1)S(1)} %get-tuple-element.14.own_ref, bf16[80,512]{1,0:T(8,128)(2,1)S(1)} %collective-permute-done.other_ref, f32[16,128]{1,0:T(8,128)S(1)} %get-tuple-element.15.facts_ref, ...), custom_call_target="tpu_custom_call" | custom-call | flops 1000000000 | bytes 2000000 | tf_op jit(solution)/shard_map/far/pallas_call | solution.py:392
  61.1 0.0 collective-permute-done.2.cross_ref
  61.1 1.1 %cross.1 = (f32[2,64,512]{2,1,0:T(8,128)S(1)}, s16[4,64,128]{2,1,0:T(8,128)(2,1)S(1)}) custom-call(bf16[80,512]{1,0:T(8,128)(2,1)S(1)} %collective-permute-done.2.cross_ref, f32[16,128]{1,0:T(8,128)S(1)} %get-tuple-element.15.facts_ref, f32[2,64,640]{2,1,0:T(8,128)S(1)} %far.1.kept_ref, bf16[128,1024]{1,0:T(8,128)(2,1)S(1)} %get-tuple-element.18.right_ref), custom_call_target="tpu_custom_call" | custom-call | flops 1000000000 | bytes 2000000 | tf_op jit(solution)/shard_map/cross/pallas_call | solution.py:401
  62.2 0.0 all-to-all-done.1.got_ref
  62.2 0.9 %depth.1 = s16[8,144,128]{2,1,0:T(8,128)(2,1)} custom-call(s16[32,16,128]{2,1,0:T(8,128)(2,1)S(1)} %all-to-all-done.1.got_ref, s16[4,64,128]{2,1,0:T(8,128)(2,1)S(1)} %get-tuple-element.21.low_ref), custom_call_target="tpu_custom_call" | custom-call | flops 100000 | bytes 500000 | tf_op jit(solution)/shard_map/depth/pallas_call | solution.py:423
  63.1 5.1 %all-to-all-start.2 = ((s16[8,144,128]{2,1,0:T(8,128)(2,1)}), s16[8,144,128]{2,1,0:T(8,128)(2,1)S(1)}, u32[]{:S(2)}, u32[]{:S(2)}) async-start(s16[8,144,128]{2,1,0:T(8,128)(2,1)} %depth.1), calls=%async_computation.2 | async-start | bytes 589824 | tf_op jit(solution)/shard_map/all_to_all | solution.py:330
  68.2 0.0 copy-start
  68.2 0.6 factor.1.factor_ref
  68.9 6.1 %all-to-all-done.2.got_ref = s16[8,144,128]{2,1,0:T(8,128)(2,1)S(1)} async-done(((s16[8,144,128]{2,1,0:T(8,128)(2,1)}), s16[8,144,128]{2,1,0:T(8,128)(2,1)S(1)}, u32[]{:S(2)}, u32[]{:S(2)}) %all-to-all-start.2) | async-done | bytes 294944 | tf_op jit(solution)/shard_map/all_to_all | solution.py:330
  75.0 0.0 copy-done
  75.0 1.8 %final.1 = f32[2,64,512]{2,1,0:T(8,128)} custom-call(s16[8,144,128]{2,1,0:T(8,128)(2,1)S(1)} %all-to-all-done.2.got_ref, bf16[2,896,512]{2,1,0:T(8,128)(2,1)S(1)} %factor.1.factor_ref, f32[128,128]{1,0:T(8,128)S(1)} %copy-done, f32[2,64,512]{2,1,0:T(8,128)S(1)} %get-tuple-element.22.diagonal_ref), custom_call_target="tpu_custom_call" | custom-call | flops 1000000000 | bytes 3000000 | tf_op jit(solution)/shard_map/final/pallas_call | solution.py:433
Async XLA Ops:
  1.7 10.2 %collective-permute-start = (bf16[80,512]{1,0:T(8,128)(2,1)S(1)}, bf16[80,512]{1,0:T(8,128)(2,1)S(1)}, u32[]{:S(2)}, u32[]{:S(2)}) collective-permute-start(bf16[80,512]{1,0:T(8,128)(2,1)S(1)} %get-tuple-element.14.own_ref), channel_id=1, source_target_pairs={{0,1},{1,0},{2,3},{3,2},{4,5},{5,4},{6,7},{7,6},{8,9},{9,8},{10,11... | collective-permute-start | bytes 245768 | tf_op jit(solution)/shard_map/ppermute | solution.py:326
  22.2 40.0 %all-to-all-start.1 = ((s16[32,16,128]{2,1,0:T(8,128)(2,1)}), s16[32,16,128]{2,1,0:T(8,128)(2,1)S(1)}, u32[]{:S(2)}, u32[]{:S(2)}) async-start(s16[32,16,128]{2,1,0:T(8,128)(2,1)} %line.1), calls=%async_computation.1 | async-start | bytes 262144 | tf_op jit(solution)/shard_map/all_to_all | solution.py:330
  36.6 18.0 %collective-permute-start.1 = (bf16[80,512]{1,0:T(8,128)(2,1)S(1)}, bf16[80,512]{1,0:T(8,128)(2,1)S(1)}, u32[]{:S(2)}, u32[]{:S(2)}) collective-permute-start(bf16[80,512]{1,0:T(8,128)(2,1)S(1)} %get-tuple-element.14.own_ref), channel_id=1, source_target_pairs={{0,2},{2,0},{1,3},{3,1},{4,6},{6,4},{5,7},{7,5},{8,10},{10,8},{9,1... | collective-permute-start | bytes 245768 | tf_op jit(solution)/shard_map/ppermute | solution.py:326
  54.6 6.5 %collective-permute-start.2 = (bf16[80,512]{1,0:T(8,128)(2,1)S(1)}, bf16[80,512]{1,0:T(8,128)(2,1)S(1)}, u32[]{:S(2)}, u32[]{:S(2)}) collective-permute-start(bf16[80,512]{1,0:T(8,128)(2,1)S(1)} %collective-permute-done.1.far_ref), channel_id=1, source_target_pairs={{0,1},{1,0},{2,3},{3,2},{4,5},{5,4},{6,7},{7,6},{8,9},{9,8},{10,11... | collective-permute-start | bytes 245768 | tf_op jit(solution)/shard_map/ppermute | solution.py:326
  63.1 11.9 %all-to-all-start.2 = ((s16[8,144,128]{2,1,0:T(8,128)(2,1)}), s16[8,144,128]{2,1,0:T(8,128)(2,1)S(1)}, u32[]{:S(2)}, u32[]{:S(2)}) async-start(s16[8,144,128]{2,1,0:T(8,128)(2,1)} %depth.1), calls=%async_computation.2 | async-start | bytes 589824 | tf_op jit(solution)/shard_map/all_to_all | solution.py:330
  68.2 6.8 %copy-start = (f32[128,128]{1,0:T(8,128)S(1)}, f32[128,128]{1,0:T(8,128)}, u32[]{:S(2)}) copy-start(f32[128,128]{1,0:T(8,128)} %coupling_ref.1) | copy-start | bytes 196612

commit v3 on v2

--- a/solution.py
+++ b/solution.py
@@ -173,11 +173,15 @@
     accumulate(own_ref, facts_ref, right_ref, held_ref, NEAR_SPANS, True)
 
 
+def scale_kernel(facts_ref, marks_ref, out_ref):
+    for level in range(LEVELS):
+        out_ref[level] = (marks_ref[level] - 0.5) * facts_ref[0:8, 0:1]
+
+
 def factor_kernel(facts_ref, marks_ref, right_ref, factor_ref):
-    inverse = facts_ref[0:8, 0:1]
     right = right_ref[:, :WIDTH]
     for level in range(LEVELS):
-        turned = left_form((marks_ref[level] - 0.5) * inverse, 0.0).T.astype(BF16)
+        turned = left_form(marks_ref[level], 0.0).T.astype(BF16)
         exponent = jnp.dot(turned, right, preferred_element_type=F32)
         for which, value in enumerate(kernel_pair(exponent, facts_ref[8:9, 0:1])):
             factor_ref[which, level * RANK : (level + 1) * RANK, :] = value.astype(BF16)
@@ -411,6 +415,15 @@
         cost_estimate=cost(10**9, 2 * 10**6),
         name="cross",
     )(cross, facts, kept, right)
+    anchors = pl.pallas_call(
+        scale_kernel,
+        out_shape=jax.ShapeDtypeStruct((LEVELS, 8, RANK), F32),
+        in_specs=[VMEM] * 2,
+        out_specs=VMEM,
+        compiler_params=ROOM,
+        cost_estimate=cost(10**5, 10**5),
+        name="scale",
+    )(facts, marks)
     factor = pl.pallas_call(
         factor_kernel,
         out_shape=jax.ShapeDtypeStruct((2, LEVELS * RANK, WIDTH), BF16),
@@ -419,7 +432,7 @@
         compiler_params=ROOM,
         cost_estimate=cost(10**9, 3 * 10**6),
         name="factor",
-    )(facts, marks, right)
+    )(facts, anchors, right)
     wide = pl.pallas_call(
         depth_kernel,
         out_shape=jax.ShapeDtypeStruct((8, PROBES + 5 * QUARTER, 128), I16),

time: 77.2 us -> 77.2 us (level)
  no operation moved by 1% of the time
where the time goes in v3:
time: 77.2 us; the launch traced here: 76.8 us
  starting transfers between devices  44.9 us (58%)
  waiting for transfers between devices  12.3 us (16%)
  Pallas kernels  10.8 us (14%)
  blocking collectives  8.03 us (10%)
    ppermute x3, starting transfers between devices, swap(): return lax.ppermute(value, axis, [(0, 1), (1, 0)])  25.4 us
    all_to_all x2, starting transfers between devices, exchange(): return lax.all_to_all(value, axes, 0, 0, tiled=True)  19.5 us
    all_to_all x1, blocking collectives, exchange(): return lax.all_to_all(value, axes, 0, 0, tiled=True)  8.03 us
    ppermute x3, waiting for transfers between devices, swap(): return lax.ppermute(value, axis, [(0, 1), (1, 0)])  6.18 us
    all_to_all x2, waiting for transfers between devices, exchange(): return lax.all_to_all(value, axes, 0, 0, tiled=True)  6.13 us
    pallas_call x1, Pallas kernels, on_device(): pl.pallas_call(final_kernel, out_shape=jax.ShapeDtypeStruct((2, PROBES, W...  1.78 us
    pallas_call x1, Pallas kernels, on_device(): pl.pallas_call(far_kernel, out_shape=jax.ShapeDtypeStruct((2, PROBES, KEP...  1.67 us
  transfers between devices with their start and end apart: 5, of which 2 were waited for; matrix products, arithmetic and copies ran while one was open for 0% of the time, Pallas kernels for 6%

profile of v3, /device:TPU:1, one launch (start us, length us, event | category | flops | bytes accessed | tf_op | source)
XLA Modules:
  0.0 76.8 jit_solution(10795678080480472111)
XLA Ops:
  0.7 1.0 %prepare.1 = (bf16[80,512]{1,0:T(8,128)(2,1)S(1)}, f32[7,8,128]{2,1,0:T(8,128)S(1)}, f32[16,128]{1,0:T(8,128)S(1)}) custom-call(s32[8,512]{1,0:T(8,128)} %coords_ref.1, f32[64,512]{1,0:T(8,128)} %probes_ref.1, f32[254,8,128]{2,1,0:T(8,128)} %marks_ref.1, f32[8]{0:T(128)} %scales_ref.1, f32[1]{0:T(128)S(6)} %copy.7.strength_ref), custom_call_target="tpu_custom_call" | custom-call | flops 100000 | bytes 200000 | tf_op jit(solution)/shard_map/prepare/pallas_call | solution.py:338
  1.7 8.7 %collective-permute-start = (bf16[80,512]{1,0:T(8,128)(2,1)S(1)}, bf16[80,512]{1,0:T(8,128)(2,1)S(1)}, u32[]{:S(2)}, u32[]{:S(2)}) collective-permute-start(bf16[80,512]{1,0:T(8,128)(2,1)S(1)} %get-tuple-element.14.own_ref), channel_id=1, source_target_pairs={{0,1},{1,0},{2,3},{3,2},{4,5},{5,4},{6,7},{7,6},{8,9},{9,8},{10,11... | collective-permute-start | bytes 245768 | tf_op jit(solution)/shard_map/ppermute | solution.py:330
  10.4 1.4 %own.1 = (f32[2,64,1024]{2,1,0:T(8,128)S(1)}, bf16[128,1024]{1,0:T(8,128)(2,1)S(1)}) custom-call(bf16[80,512]{1,0:T(8,128)(2,1)S(1)} %get-tuple-element.14.own_ref, f32[16,128]{1,0:T(8,128)S(1)} %get-tuple-element.15.facts_ref, f32[7,8,128]{2,1,0:T(8,128)S(1)} %get-tuple-element.16.marks_ref), custom_call_target="tpu_custom_call" | custom-call | flops 1000000000 | bytes 2000000 | tf_op jit(solution)/shard_map/own/pallas_call | solution.py:359
  11.9 0.0 collective-permute-done.other_ref
  11.9 1.5 %near.1 = (f32[2,64,128]{2,1,0:T(8,128)S(1)}, s16[8,80,128]{2,1,0:T(8,128)(2,1)S(1)}) custom-call(bf16[80,512]{1,0:T(8,128)(2,1)S(1)} %collective-permute-done.other_ref, f32[16,128]{1,0:T(8,128)S(1)} %get-tuple-element.15.facts_ref, f32[2,64,1024]{2,1,0:T(8,128)S(1)} %get-tuple-element.17.held_ref, bf16[128,1024]{1,0:T(8,128)(2,1)S(1)} %get-tuple-element.18.right_ref), custom_call_target="tpu_custom_call" | custom-call | flops 1000000000 | bytes 2000000 | tf_op jit(solution)/shard_map/near/pallas_call | solution.py:371
  13.4 8.0 %all_to_all.15.got_ref = s16[8,80,128]{2,1,0:T(8,128)(2,1)S(1)} all-to-all(s16[8,80,128]{2,1,0:T(8,128)(2,1)S(1)} %get-tuple-element.19), channel_id=1, replica_groups=mesh['x'=4,'zh'=4,'zl'=2,'y'=4,'h'=2,'c'=2] {'zl','y'}, dimensions={0} | all-to-all | bytes 327680 | tf_op jit(solution)/shard_map/all_to_all | solution.py:334
  21.4 0.8 %line.1 = s16[32,16,128]{2,1,0:T(8,128)(2,1)} custom-call(s16[8,80,128]{2,1,0:T(8,128)(2,1)S(1)} %all_to_all.15.got_ref), custom_call_target="tpu_custom_call" | custom-call | flops 100000 | bytes 300000 | tf_op jit(solution)/shard_map/line/pallas_call | solution.py:385
  22.2 14.3 %all-to-all-start.1 = ((s16[32,16,128]{2,1,0:T(8,128)(2,1)}), s16[32,16,128]{2,1,0:T(8,128)(2,1)S(1)}, u32[]{:S(2)}, u32[]{:S(2)}) async-start(s16[32,16,128]{2,1,0:T(8,128)(2,1)} %line.1), calls=%async_computation.1 | async-start | bytes 262144 | tf_op jit(solution)/shard_map/all_to_all | solution.py:334
  36.6 11.9 %collective-permute-start.1 = (bf16[80,512]{1,0:T(8,128)(2,1)S(1)}, bf16[80,512]{1,0:T(8,128)(2,1)S(1)}, u32[]{:S(2)}, u32[]{:S(2)}) collective-permute-start(bf16[80,512]{1,0:T(8,128)(2,1)S(1)} %get-tuple-element.14.own_ref), channel_id=1, source_target_pairs={{0,2},{2,0},{1,3},{3,1},{4,6},{6,4},{5,7},{7,5},{8,10},{10,8},{9,1... | collective-permute-start | bytes 245768 | tf_op jit(solution)/shard_map/ppermute | solution.py:330
  48.5 6.2 %collective-permute-done.1.far_ref = bf16[80,512]{1,0:T(8,128)(2,1)S(1)} collective-permute-done((bf16[80,512]{1,0:T(8,128)(2,1)S(1)}, bf16[80,512]{1,0:T(8,128)(2,1)S(1)}, u32[]{:S(2)}, u32[]{:S(2)}) %collective-permute-start.1) | collective-permute-done | bytes 81952 | tf_op jit(solution)/shard_map/ppermute | solution.py:330
  54.6 4.8 %collective-permute-start.2 = (bf16[80,512]{1,0:T(8,128)(2,1)S(1)}, bf16[80,512]{1,0:T(8,128)(2,1)S(1)}, u32[]{:S(2)}, u32[]{:S(2)}) collective-permute-start(bf16[80,512]{1,0:T(8,128)(2,1)S(1)} %collective-permute-done.1.far_ref), channel_id=1, source_target_pairs={{0,1},{1,0},{2,3},{3,2},{4,5},{5,4},{6,7},{7,6},{8,9},{9,8},{10,11... | collective-permute-start | bytes 245768 | tf_op jit(solution)/shard_map/ppermute | solution.py:330
  59.4 1.7 %far.1.kept_ref = f32[2,64,640]{2,1,0:T(8,128)S(1)} custom-call(bf16[80,512]{1,0:T(8,128)(2,1)S(1)} %collective-permute-done.1.far_ref, bf16[80,512]{1,0:T(8,128)(2,1)S(1)} %get-tuple-element.14.own_ref, bf16[80,512]{1,0:T(8,128)(2,1)S(1)} %collective-permute-done.other_ref, f32[16,128]{1,0:T(8,128)S(1)} %get-tuple-element.15.facts_ref, ...), custom_call_target="tpu_custom_call" | custom-call | flops 1000000000 | bytes 2000000 | tf_op jit(solution)/shard_map/far/pallas_call | solution.py:396
  61.1 0.0 collective-permute-done.2.cross_ref
  61.1 1.1 %cross.1 = (f32[2,64,512]{2,1,0:T(8,128)S(1)}, s16[4,64,128]{2,1,0:T(8,128)(2,1)S(1)}) custom-call(bf16[80,512]{1,0:T(8,128)(2,1)S(1)} %collective-permute-done.2.cross_ref, f32[16,128]{1,0:T(8,128)S(1)} %get-tuple-element.15.facts_ref, f32[2,64,640]{2,1,0:T(8,128)S(1)} %far.1.kept_ref, bf16[128,1024]{1,0:T(8,128)(2,1)S(1)} %get-tuple-element.18.right_ref), custom_call_target="tpu_custom_call" | custom-call | flops 1000000000 | bytes 2000000 | tf_op jit(solution)/shard_map/cross/pallas_call | solution.py:405
  62.2 0.0 all-to-all-done.1.got_ref
  62.2 0.9 %depth.1 = s16[8,144,128]{2,1,0:T(8,128)(2,1)} custom-call(s16[32,16,128]{2,1,0:T(8,128)(2,1)S(1)} %all-to-all-done.1.got_ref, s16[4,64,128]{2,1,0:T(8,128)(2,1)S(1)} %get-tuple-element.21.low_ref), custom_call_target="tpu_custom_call" | custom-call | flops 100000 | bytes 500000 | tf_op jit(solution)/shard_map/depth/pallas_call | solution.py:436
  63.1 5.1 %all-to-all-start.2 = ((s16[8,144,128]{2,1,0:T(8,128)(2,1)}), s16[8,144,128]{2,1,0:T(8,128)(2,1)S(1)}, u32[]{:S(2)}, u32[]{:S(2)}) async-start(s16[8,144,128]{2,1,0:T(8,128)(2,1)} %depth.1), calls=%async_computation.2 | async-start | bytes 589824 | tf_op jit(solution)/shard_map/all_to_all | solution.py:334
  68.2 0.1 scale.1.marks_ref
  68.3 0.0 copy-start
  68.3 0.6 factor.1.factor_ref
  68.9 6.1 %all-to-all-done.2.got_ref = s16[8,144,128]{2,1,0:T(8,128)(2,1)S(1)} async-done(((s16[8,144,128]{2,1,0:T(8,128)(2,1)}), s16[8,144,128]{2,1,0:T(8,128)(2,1)S(1)}, u32[]{:S(2)}, u32[]{:S(2)}) %all-to-all-start.2) | async-done | bytes 294944 | tf_op jit(solution)/shard_map/all_to_all | solution.py:334
  75.0 0.0 copy-done
  75.0 1.8 %final.1 = f32[2,64,512]{2,1,0:T(8,128)} custom-call(s16[8,144,128]{2,1,0:T(8,128)(2,1)S(1)} %all-to-all-done.2.got_ref, bf16[2,896,512]{2,1,0:T(8,128)(2,1)S(1)} %factor.1.factor_ref, f32[128,128]{1,0:T(8,128)S(1)} %copy-done, f32[2,64,512]{2,1,0:T(8,128)S(1)} %get-tuple-element.22.diagonal_ref), custom_call_target="tpu_custom_call" | custom-call | flops 1000000000 | bytes 3000000 | tf_op jit(solution)/shard_map/final/pallas_call | solution.py:446
Async XLA Ops:
  1.7 10.2 %collective-permute-start = (bf16[80,512]{1,0:T(8,128)(2,1)S(1)}, bf16[80,512]{1,0:T(8,128)(2,1)S(1)}, u32[]{:S(2)}, u32[]{:S(2)}) collective-permute-start(bf16[80,512]{1,0:T(8,128)(2,1)S(1)} %get-tuple-element.14.own_ref), channel_id=1, source_target_pairs={{0,1},{1,0},{2,3},{3,2},{4,5},{5,4},{6,7},{7,6},{8,9},{9,8},{10,11... | collective-permute-start | bytes 245768 | tf_op jit(solution)/shard_map/ppermute | solution.py:330
  22.2 40.0 %all-to-all-start.1 = ((s16[32,16,128]{2,1,0:T(8,128)(2,1)}), s16[32,16,128]{2,1,0:T(8,128)(2,1)S(1)}, u32[]{:S(2)}, u32[]{:S(2)}) async-start(s16[32,16,128]{2,1,0:T(8,128)(2,1)} %line.1), calls=%async_computation.1 | async-start | bytes 262144 | tf_op jit(solution)/shard_map/all_to_all | solution.py:334
  36.6 18.0 %collective-permute-start.1 = (bf16[80,512]{1,0:T(8,128)(2,1)S(1)}, bf16[80,512]{1,0:T(8,128)(2,1)S(1)}, u32[]{:S(2)}, u32[]{:S(2)}) collective-permute-start(bf16[80,512]{1,0:T(8,128)(2,1)S(1)} %get-tuple-element.14.own_ref), channel_id=1, source_target_pairs={{0,2},{2,0},{1,3},{3,1},{4,6},{6,4},{5,7},{7,5},{8,10},{10,8},{9,1... | collective-permute-start | bytes 245768 | tf_op jit(solution)/shard_map/ppermute | solution.py:330
  54.6 6.5 %collective-permute-start.2 = (bf16[80,512]{1,0:T(8,128)(2,1)S(1)}, bf16[80,512]{1,0:T(8,128)(2,1)S(1)}, u32[]{:S(2)}, u32[]{:S(2)}) collective-permute-start(bf16[80,512]{1,0:T(8,128)(2,1)S(1)} %collective-permute-done.1.far_ref), channel_id=1, source_target_pairs={{0,1},{1,0},{2,3},{3,2},{4,5},{5,4},{6,7},{7,6},{8,9},{9,8},{10,11... | collective-permute-start | bytes 245768 | tf_op jit(solution)/shard_map/ppermute | solution.py:330
  63.1 11.9 %all-to-all-start.2 = ((s16[8,144,128]{2,1,0:T(8,128)(2,1)}), s16[8,144,128]{2,1,0:T(8,128)(2,1)S(1)}, u32[]{:S(2)}, u32[]{:S(2)}) async-start(s16[8,144,128]{2,1,0:T(8,128)(2,1)} %depth.1), calls=%async_computation.2 | async-start | bytes 589824 | tf_op jit(solution)/shard_map/all_to_all | solution.py:334
  68.3 6.7 %copy-start = (f32[128,128]{1,0:T(8,128)S(1)}, f32[128,128]{1,0:T(8,128)}, u32[]{:S(2)}) copy-start(f32[128,128]{1,0:T(8,128)} %coupling_ref.1) | copy-start | bytes 196612

commit v4 on v3

--- a/solution.py
+++ b/solution.py
@@ -19,7 +19,8 @@
 LANES = 1024
 BLOCK = 256
 KEPT = WIDTH + RANK
-NEAR_SPANS = ((512, 768), (768, 1024))
+USED = WIDTH + LEVELS * HALF
+NEAR_SPANS = ((512, 768), (768, USED))
 SELF_SPANS = ((0, 256), (256, 512))
 LATE_SPANS = ((0, 256), (256, 512), (512, 640))
 ROOT = math.sqrt(math.log2(math.e))
@@ -189,7 +190,7 @@
 
 def near_kernel(other_ref, facts_ref, held_ref, right_ref, kept_ref, line_ref, sums):
     zl = lax.axis_index("zl")
-    sums[:, :, WIDTH:] = held_ref[:, :, WIDTH:]
+    sums[:, :, WIDTH:USED] = held_ref[:, :, WIDTH:USED]
     accumulate(other_ref, facts_ref, right_ref, sums, NEAR_SPANS, False)
     kept_ref[...] = sums[:, :, WIDTH:KEPT]
     units = [unit_of(sums, level) for level in range(2, LEVELS)]

time: 77.2 us -> 77.2 us (level)
  no operation moved by 1% of the time
where the time goes in v4:
time: 77.2 us; the launch traced here: 76.8 us
  starting transfers between devices  44.8 us (58%)
  waiting for transfers between devices  12.3 us (16%)
  Pallas kernels  10.9 us (14%)
  blocking collectives  8.03 us (10%)
    ppermute x3, starting transfers between devices, swap(): return lax.ppermute(value, axis, [(0, 1), (1, 0)])  25.4 us
    all_to_all x2, starting transfers between devices, exchange(): return lax.all_to_all(value, axes, 0, 0, tiled=True)  19.4 us
    all_to_all x1, blocking collectives, exchange(): return lax.all_to_all(value, axes, 0, 0, tiled=True)  8.03 us
    ppermute x3, waiting for transfers between devices, swap(): return lax.ppermute(value, axis, [(0, 1), (1, 0)])  6.18 us
    all_to_all x2, waiting for transfers between devices, exchange(): return lax.all_to_all(value, axes, 0, 0, tiled=True)  6.13 us
    pallas_call x1, Pallas kernels, on_device(): pl.pallas_call(final_kernel, out_shape=jax.ShapeDtypeStruct((2, PROBES, W...  1.78 us
    pallas_call x1, Pallas kernels, on_device(): pl.pallas_call(far_kernel, out_shape=jax.ShapeDtypeStruct((2, PROBES, KEP...  1.68 us
  transfers between devices with their start and end apart: 5, of which 2 were waited for; matrix products, arithmetic and copies ran while one was open for 0% of the time, Pallas kernels for 6%

profile of v4, /device:TPU:1, one launch (start us, length us, event | category | flops | bytes accessed | tf_op | source)
XLA Modules:
  0.0 76.8 jit_solution(15690804116092294003)
XLA Ops:
  0.7 1.0 %prepare.1 = (bf16[80,512]{1,0:T(8,128)(2,1)S(1)}, f32[7,8,128]{2,1,0:T(8,128)S(1)}, f32[16,128]{1,0:T(8,128)S(1)}) custom-call(s32[8,512]{1,0:T(8,128)} %coords_ref.1, f32[64,512]{1,0:T(8,128)} %probes_ref.1, f32[254,8,128]{2,1,0:T(8,128)} %marks_ref.1, f32[8]{0:T(128)} %scales_ref.1, f32[1]{0:T(128)S(6)} %copy.7.strength_ref), custom_call_target="tpu_custom_call" | custom-call | flops 100000 | bytes 200000 | tf_op jit(solution)/shard_map/prepare/pallas_call | solution.py:339
  1.7 8.7 %collective-permute-start = (bf16[80,512]{1,0:T(8,128)(2,1)S(1)}, bf16[80,512]{1,0:T(8,128)(2,1)S(1)}, u32[]{:S(2)}, u32[]{:S(2)}) collective-permute-start(bf16[80,512]{1,0:T(8,128)(2,1)S(1)} %get-tuple-element.14.own_ref), channel_id=1, source_target_pairs={{0,1},{1,0},{2,3},{3,2},{4,5},{5,4},{6,7},{7,6},{8,9},{9,8},{10,11... | collective-permute-start | bytes 245768 | tf_op jit(solution)/shard_map/ppermute | solution.py:331
  10.4 1.5 %own.1 = (f32[2,64,1024]{2,1,0:T(8,128)S(1)}, bf16[128,1024]{1,0:T(8,128)(2,1)S(1)}) custom-call(bf16[80,512]{1,0:T(8,128)(2,1)S(1)} %get-tuple-element.14.own_ref, f32[16,128]{1,0:T(8,128)S(1)} %get-tuple-element.15.facts_ref, f32[7,8,128]{2,1,0:T(8,128)S(1)} %get-tuple-element.16.marks_ref), custom_call_target="tpu_custom_call" | custom-call | flops 1000000000 | bytes 2000000 | tf_op jit(solution)/shard_map/own/pallas_call | solution.py:360
  11.9 0.0 collective-permute-done.other_ref
  11.9 1.5 %near.1 = (f32[2,64,128]{2,1,0:T(8,128)S(1)}, s16[8,80,128]{2,1,0:T(8,128)(2,1)S(1)}) custom-call(bf16[80,512]{1,0:T(8,128)(2,1)S(1)} %collective-permute-done.other_ref, f32[16,128]{1,0:T(8,128)S(1)} %get-tuple-element.15.facts_ref, f32[2,64,1024]{2,1,0:T(8,128)S(1)} %get-tuple-element.17.held_ref, bf16[128,1024]{1,0:T(8,128)(2,1)S(1)} %get-tuple-element.18.right_ref), custom_call_target="tpu_custom_call" | custom-call | flops 1000000000 | bytes 2000000 | tf_op jit(solution)/shard_map/near/pallas_call | solution.py:372
  13.4 8.0 %all_to_all.15.got_ref = s16[8,80,128]{2,1,0:T(8,128)(2,1)S(1)} all-to-all(s16[8,80,128]{2,1,0:T(8,128)(2,1)S(1)} %get-tuple-element.19), channel_id=1, replica_groups=mesh['x'=4,'zh'=4,'zl'=2,'y'=4,'h'=2,'c'=2] {'zl','y'}, dimensions={0} | all-to-all | bytes 327680 | tf_op jit(solution)/shard_map/all_to_all | solution.py:335
  21.5 0.8 %line.1 = s16[32,16,128]{2,1,0:T(8,128)(2,1)} custom-call(s16[8,80,128]{2,1,0:T(8,128)(2,1)S(1)} %all_to_all.15.got_ref), custom_call_target="tpu_custom_call" | custom-call | flops 100000 | bytes 300000 | tf_op jit(solution)/shard_map/line/pallas_call | solution.py:386
  22.3 14.3 %all-to-all-start.1 = ((s16[32,16,128]{2,1,0:T(8,128)(2,1)}), s16[32,16,128]{2,1,0:T(8,128)(2,1)S(1)}, u32[]{:S(2)}, u32[]{:S(2)}) async-start(s16[32,16,128]{2,1,0:T(8,128)(2,1)} %line.1), calls=%async_computation.1 | async-start | bytes 262144 | tf_op jit(solution)/shard_map/all_to_all | solution.py:335
  36.6 11.9 %collective-permute-start.1 = (bf16[80,512]{1,0:T(8,128)(2,1)S(1)}, bf16[80,512]{1,0:T(8,128)(2,1)S(1)}, u32[]{:S(2)}, u32[]{:S(2)}) collective-permute-start(bf16[80,512]{1,0:T(8,128)(2,1)S(1)} %get-tuple-element.14.own_ref), channel_id=1, source_target_pairs={{0,2},{2,0},{1,3},{3,1},{4,6},{6,4},{5,7},{7,5},{8,10},{10,8},{9,1... | collective-permute-start | bytes 245768 | tf_op jit(solution)/shard_map/ppermute | solution.py:331
  48.5 6.2 %collective-permute-done.1.far_ref = bf16[80,512]{1,0:T(8,128)(2,1)S(1)} collective-permute-done((bf16[80,512]{1,0:T(8,128)(2,1)S(1)}, bf16[80,512]{1,0:T(8,128)(2,1)S(1)}, u32[]{:S(2)}, u32[]{:S(2)}) %collective-permute-start.1) | collective-permute-done | bytes 81952 | tf_op jit(solution)/shard_map/ppermute | solution.py:331
  54.6 4.8 %collective-permute-start.2 = (bf16[80,512]{1,0:T(8,128)(2,1)S(1)}, bf16[80,512]{1,0:T(8,128)(2,1)S(1)}, u32[]{:S(2)}, u32[]{:S(2)}) collective-permute-start(bf16[80,512]{1,0:T(8,128)(2,1)S(1)} %collective-permute-done.1.far_ref), channel_id=1, source_target_pairs={{0,1},{1,0},{2,3},{3,2},{4,5},{5,4},{6,7},{7,6},{8,9},{9,8},{10,11... | collective-permute-start | bytes 245768 | tf_op jit(solution)/shard_map/ppermute | solution.py:331
  59.5 1.7 %far.1.kept_ref = f32[2,64,640]{2,1,0:T(8,128)S(1)} custom-call(bf16[80,512]{1,0:T(8,128)(2,1)S(1)} %collective-permute-done.1.far_ref, bf16[80,512]{1,0:T(8,128)(2,1)S(1)} %get-tuple-element.14.own_ref, bf16[80,512]{1,0:T(8,128)(2,1)S(1)} %collective-permute-done.other_ref, f32[16,128]{1,0:T(8,128)S(1)} %get-tuple-element.15.facts_ref, ...), custom_call_target="tpu_custom_call" | custom-call | flops 1000000000 | bytes 2000000 | tf_op jit(solution)/shard_map/far/pallas_call | solution.py:397
  61.1 0.0 collective-permute-done.2.cross_ref
  61.2 1.1 %cross.1 = (f32[2,64,512]{2,1,0:T(8,128)S(1)}, s16[4,64,128]{2,1,0:T(8,128)(2,1)S(1)}) custom-call(bf16[80,512]{1,0:T(8,128)(2,1)S(1)} %collective-permute-done.2.cross_ref, f32[16,128]{1,0:T(8,128)S(1)} %get-tuple-element.15.facts_ref, f32[2,64,640]{2,1,0:T(8,128)S(1)} %far.1.kept_ref, bf16[128,1024]{1,0:T(8,128)(2,1)S(1)} %get-tuple-element.18.right_ref), custom_call_target="tpu_custom_call" | custom-call | flops 1000000000 | bytes 2000000 | tf_op jit(solution)/shard_map/cross/pallas_call | solution.py:406
  62.3 0.0 all-to-all-done.1.got_ref
  62.3 0.9 %depth.1 = s16[8,144,128]{2,1,0:T(8,128)(2,1)} custom-call(s16[32,16,128]{2,1,0:T(8,128)(2,1)S(1)} %all-to-all-done.1.got_ref, s16[4,64,128]{2,1,0:T(8,128)(2,1)S(1)} %get-tuple-element.21.low_ref), custom_call_target="tpu_custom_call" | custom-call | flops 100000 | bytes 500000 | tf_op jit(solution)/shard_map/depth/pallas_call | solution.py:437
  63.1 5.1 %all-to-all-start.2 = ((s16[8,144,128]{2,1,0:T(8,128)(2,1)}), s16[8,144,128]{2,1,0:T(8,128)(2,1)S(1)}, u32[]{:S(2)}, u32[]{:S(2)}) async-start(s16[8,144,128]{2,1,0:T(8,128)(2,1)} %depth.1), calls=%async_computation.2 | async-start | bytes 589824 | tf_op jit(solution)/shard_map/all_to_all | solution.py:335
  68.2 0.1 scale.1.marks_ref
  68.3 0.0 copy-start
  68.3 0.6 factor.1.factor_ref
  68.9 6.1 %all-to-all-done.2.got_ref = s16[8,144,128]{2,1,0:T(8,128)(2,1)S(1)} async-done(((s16[8,144,128]{2,1,0:T(8,128)(2,1)}), s16[8,144,128]{2,1,0:T(8,128)(2,1)S(1)}, u32[]{:S(2)}, u32[]{:S(2)}) %all-to-all-start.2) | async-done | bytes 294944 | tf_op jit(solution)/shard_map/all_to_all | solution.py:335
  75.0 0.0 copy-done
  75.0 1.8 %final.1 = f32[2,64,512]{2,1,0:T(8,128)} custom-call(s16[8,144,128]{2,1,0:T(8,128)(2,1)S(1)} %all-to-all-done.2.got_ref, bf16[2,896,512]{2,1,0:T(8,128)(2,1)S(1)} %factor.1.factor_ref, f32[128,128]{1,0:T(8,128)S(1)} %copy-done, f32[2,64,512]{2,1,0:T(8,128)S(1)} %get-tuple-element.22.diagonal_ref), custom_call_target="tpu_custom_call" | custom-call | flops 1000000000 | bytes 3000000 | tf_op jit(solution)/shard_map/final/pallas_call | solution.py:447
Async XLA Ops:
  1.7 10.2 %collective-permute-start = (bf16[80,512]{1,0:T(8,128)(2,1)S(1)}, bf16[80,512]{1,0:T(8,128)(2,1)S(1)}, u32[]{:S(2)}, u32[]{:S(2)}) collective-permute-start(bf16[80,512]{1,0:T(8,128)(2,1)S(1)} %get-tuple-element.14.own_ref), channel_id=1, source_target_pairs={{0,1},{1,0},{2,3},{3,2},{4,5},{5,4},{6,7},{7,6},{8,9},{9,8},{10,11... | collective-permute-start | bytes 245768 | tf_op jit(solution)/shard_map/ppermute | solution.py:331
  22.3 40.0 %all-to-all-start.1 = ((s16[32,16,128]{2,1,0:T(8,128)(2,1)}), s16[32,16,128]{2,1,0:T(8,128)(2,1)S(1)}, u32[]{:S(2)}, u32[]{:S(2)}) async-start(s16[32,16,128]{2,1,0:T(8,128)(2,1)} %line.1), calls=%async_computation.1 | async-start | bytes 262144 | tf_op jit(solution)/shard_map/all_to_all | solution.py:335
  36.6 18.0 %collective-permute-start.1 = (bf16[80,512]{1,0:T(8,128)(2,1)S(1)}, bf16[80,512]{1,0:T(8,128)(2,1)S(1)}, u32[]{:S(2)}, u32[]{:S(2)}) collective-permute-start(bf16[80,512]{1,0:T(8,128)(2,1)S(1)} %get-tuple-element.14.own_ref), channel_id=1, source_target_pairs={{0,2},{2,0},{1,3},{3,1},{4,6},{6,4},{5,7},{7,5},{8,10},{10,8},{9,1... | collective-permute-start | bytes 245768 | tf_op jit(solution)/shard_map/ppermute | solution.py:331
  54.6 6.5 %collective-permute-start.2 = (bf16[80,512]{1,0:T(8,128)(2,1)S(1)}, bf16[80,512]{1,0:T(8,128)(2,1)S(1)}, u32[]{:S(2)}, u32[]{:S(2)}) collective-permute-start(bf16[80,512]{1,0:T(8,128)(2,1)S(1)} %collective-permute-done.1.far_ref), channel_id=1, source_target_pairs={{0,1},{1,0},{2,3},{3,2},{4,5},{5,4},{6,7},{7,6},{8,9},{9,8},{10,11... | collective-permute-start | bytes 245768 | tf_op jit(solution)/shard_map/ppermute | solution.py:331
  63.1 11.9 %all-to-all-start.2 = ((s16[8,144,128]{2,1,0:T(8,128)(2,1)}), s16[8,144,128]{2,1,0:T(8,128)(2,1)S(1)}, u32[]{:S(2)}, u32[]{:S(2)}) async-start(s16[8,144,128]{2,1,0:T(8,128)(2,1)} %depth.1), calls=%async_computation.2 | async-start | bytes 589824 | tf_op jit(solution)/shard_map/all_to_all | solution.py:335
  68.3 6.7 %copy-start = (f32[128,128]{1,0:T(8,128)S(1)}, f32[128,128]{1,0:T(8,128)}, u32[]{:S(2)}) copy-start(f32[128,128]{1,0:T(8,128)} %coupling_ref.1) | copy-start | bytes 196612
